TPU v7x, 32 devices: a whole 2x2x4 slice. The times are simulated.
32 devices in a mesh: section: 2 (over core), dp: 4 (over y, x), tensor: 4 (over z).
Axes of the slice: x: 2, y: 2, z: 4, core: 2. Of those that a mesh axis runs over, the one named last changes fastest.
Arguments:
- tokens_in: bfloat16 [512, 8192], P('dp', ('section', 'tensor')), may hold values from -70 to 70
- gain_attn: bfloat16 [8192], replicated, may hold values from 0.5 to 1.5
- w_query: bfloat16 [8192, 8192], P(None, ('section', 'tensor')), may hold values from -6 to 6
- w_keyval: bfloat16 [8192, 2048], P(None, ('section', 'tensor')), may hold values from -0.0625 to 0.0625
- w_out: bfloat16 [8192, 8192], P(('section', 'tensor')), may hold values from -0.0625 to 0.0625
- gain_mlp: bfloat16 [8192], replicated, may hold values from 0.5 to 1.5
- w_gate: bfloat16 [8192, 16384], P('dp', ('section', 'tensor')), may hold values from -0.0625 to 0.0625
- w_up: bfloat16 [8192, 16384], P('dp', ('section', 'tensor')), may hold values from -0.0625 to 0.0625
- w_down: bfloat16 [16384, 8192], P(('section', 'tensor'), 'dp'), may hold values from -0.046875 to 0.046875
Outputs:
- layer_out: bfloat16 [512, 8192], P(('section', 'tensor'), 'dp')
All inputs are finite; a program needn't handle non-finite values.
Results may differ from a plain program's by a relative error of at most 0.0068.
Values may be sent and summed in bfloat16 or wider, within the bound.
A program may use at most 128 MiB of HBM per device.

v0:
```python
import jax
import jax.numpy as jnp
from jax import lax
from jax.experimental import pallas as pl
from jax.experimental.pallas import tpu as pltpu
from jax.sharding import PartitionSpec as P

H = 64
KVH = 8
HD = 128
EPS = 1e-05
THETA = 10000.0
CHUNKS = 8
MESH = pl.DeviceIdType.MESH
F32 = jnp.float32
BF16 = jnp.bfloat16
VMEM = pl.BlockSpec(memory_space=pltpu.VMEM)
ANY = pl.BlockSpec(memory_space=pl.ANY)


def greet(peers):
    barrier = pltpu.get_barrier_semaphore()
    for peer in peers:
        pl.semaphore_signal(barrier, inc=1, device_id=peer, device_id_type=MESH)
    pl.semaphore_wait(barrier, len(peers))


def push(src, dst, sems, slot, device):
    return pltpu.make_async_remote_copy(
        src_ref=src,
        dst_ref=dst,
        send_sem=sems.at[0, slot],
        recv_sem=sems.at[1, slot],
        device_id=device,
        device_id_type=MESH,
    )


def others(axis):
    size = lax.axis_size(axis)
    me = lax.axis_index(axis)
    return [(step, lax.rem(me + step, size), lax.rem(me + size - step, size)) for step in range(1, size)]


def gather_group(out, at, sem_t, sem_s, on_block=lambda section, tensor, order: None):
    section, tensor = lax.axis_index("section"), lax.axis_index("tensor")
    sections, tensors = others("section"), others("tensor")
    size_t = lax.axis_size("tensor")
    started = []

    def pass_on(block_t, slot):
        for step, to, _ in sections:
            block = out.at[at(section, block_t)]
            copy = push(block, block, sem_s, slot * len(sections) + step - 1, {"section": to})
            copy.start()
            started.append(copy)

    for step, to, _ in tensors:
        block = out.at[at(section, tensor)]
        copy = push(block, block, sem_t, step - 1, {"tensor": to})
        copy.start()
        started.append(copy)
    pass_on(tensor, 0)
    on_block(section, tensor, 0)

    def from_sections(slot):
        for step, to, source in sections:
            source_t = lax.rem(tensor + size_t - slot, size_t)
            block = out.at[at(source, source_t)]
            push(block, block, sem_s, slot * len(sections) + step - 1, {"section": to}).wait_recv()
            on_block(source, source_t, (slot + 1) * len(sections) + slot + step - 1)

    for step, to, source in tensors:
        if step == 1:
            from_sections(0)
        block = out.at[at(section, source)]
        push(block, block, sem_t, step - 1, {"tensor": to}).wait_recv()
        pass_on(source, step)
        on_block(section, source, step * (len(sections) + 1))
        if step > 1:
            from_sections(step - 1)
    from_sections(size_t - 1)
    for copy in started:
        copy.wait_send()


def group_peers():
    return [{"tensor": to} for _, to, _ in others("tensor")] + [
        {"section": to} for _, to, _ in others("section")
    ]


def dma_sems(count):
    return pltpu.SemaphoreType.DMA((2, max(1, count)))


def block_order():
    section, tensor = lax.axis_index("section"), lax.axis_index("tensor")
    size_t = lax.axis_size("tensor")

    def from_sections(slot):
        return [(source, lax.rem(tensor + size_t - slot, size_t)) for _, _, source in others("section")]

    order = [(section, tensor)] + from_sections(0)
    for step, _, source in others("tensor"):
        order.append((section, source))
        if step > 1:
            order += from_sections(step - 1)
    return order + from_sections(size_t - 1)


def front_body(
    x_ref, gain_ref, cos_ref, sin_ref, wq_hbm, wk_hbm, att_ref, full_ref,
    blocks, wq, wk, qacc, kacc, stat, kv_src, kv_dst,
    sem_w, sem_own, sem_t, sem_s, sem_kv, sem_kv_out,
):
    section, tensor, me = lax.axis_index("section"), lax.axis_index("tensor"), lax.axis_index("dp")
    size_s, size_t, size_d = lax.axis_size("section"), lax.axis_size("tensor"), lax.axis_size("dp")
    count = size_s * size_t
    index = section * size_t + tensor
    local_rows, width = x_ref.shape
    features = count * width
    heads_dev = qacc.shape[1] // HD
    group_size = H // KVH
    units, _, unit = kv_src.shape
    pieces = HD // unit
    rep = group_size // heads_dev

    order = block_order()
    loads = []
    for k, (s, t) in enumerate(order):
        rows = pl.ds(pl.multiple_of((s * size_t + t) * width, width), width)
        loads.append(
            (
                pltpu.make_async_copy(wq_hbm.at[rows], wq.at[k], sem_w.at[0, k]),
                pltpu.make_async_copy(wk_hbm.at[rows], wk.at[k], sem_w.at[1, k]),
            )
        )
    for pair in loads:
        for load in pair:
            load.start()
    own = pltpu.make_async_copy(x_ref, blocks.at[index], sem_own)
    own.start()

    dps = others("dp")
    everyone = []
    for hop_s in range(size_s):
        for hop_t in range(size_t):
            for hop_d in range(size_d):
                if hop_s + hop_t + hop_d:
                    everyone.append(
                        {
                            "section": lax.rem(section + hop_s, size_s),
                            "tensor": lax.rem(tensor + hop_t, size_t),
                            "dp": lax.rem(me + hop_d, size_d),
                        }
                    )
    greet(everyone)
    own.wait()

    seen = []

    def on_block(s, t, _):
        k = len(seen)
        seen.append(k)
        for load in loads[k]:
            load.wait()
        at = s * size_t + t
        raw = blocks[at]
        full_ref[:, pl.ds(pl.multiple_of(at * width, width), width)] = raw
        rows = raw.astype(F32)
        part = jnp.sum(rows * rows, axis=-1, keepdims=True)
        stat[...] = part if k == 0 else stat[...] + part
        scaled = (rows * gain_ref[at].astype(F32)).astype(BF16)
        tile = tile_of(qacc.shape[1], 256)

        @pl.loop(0, qacc.shape[1] // tile)
        def _(j):
            cols = pl.ds(pl.multiple_of(j * tile, tile), tile)
            term = jnp.dot(scaled, wq[k, :, cols], preferred_element_type=F32)
            qacc[:, cols] = term if k == 0 else qacc[:, cols] + term

        term = jnp.dot(scaled, wk[k], preferred_element_type=F32)
        kacc[...] = term if k == 0 else kacc[...] + term

    gather_group(blocks, lambda s, t: s * size_t + t, sem_t, sem_s, on_block)
    factor = lax.rsqrt(stat[...] * (1.0 / features) + EPS)

    for i in range(units):
        kv_src[i] = (kacc[:, i * unit : (i + 1) * unit] * factor).astype(BF16)

    def dp_rows(at):
        return pl.ds(pl.multiple_of(at * local_rows, local_rows), local_rows)

    half = KVH * pieces

    def kv_copy(i, r, g, kind, piece, step, to):
        return pltpu.make_async_remote_copy(
            src_ref=kv_src.at[i],
            dst_ref=kv_dst.at[kind, piece, dp_rows(me)],
            send_sem=sem_kv_out.at[(i * rep + r) * size_d + step],
            recv_sem=sem_kv.at[1, (kind * pieces + piece) * size_d + step],
            device_id={"section": g // size_t, "tensor": lax.rem(g, size_t), "dp": to},
            device_id_type=MESH,
        )

    hops = [(step, to, source) for step, to, source in dps] + [(0, me, me)]

    def each_send(act):
        for i in range(units):
            u = index * units + i
            kind, piece = u // half, lax.rem(u, pieces)
            head = lax.rem(u, half) // pieces
            for r in range(rep):
                g = head * rep + r
                for step, to, _ in hops:
                    if step:
                        act(kv_copy(i, r, g, kind, piece, step, to), i, kind, piece, False)
                    else:
                        @pl.when(g != index)
                        def _():
                            act(kv_copy(i, r, g, kind, piece, step, to), i, kind, piece, False)

                        @pl.when(g == index)
                        def _():
                            act(None, i, kind, piece, True)

    def begin(copy, i, kind, piece, local):
        if local:
            kv_dst[kind, piece, dp_rows(me), :] = kv_src[i]
        else:
            copy.start()

    each_send(begin)

    cosine, sine = cos_ref[dp_rows(me), :], sin_ref[dp_rows(me), :]
    queries = []
    for h in range(heads_dev):
        q = qacc[:, h * HD : (h + 1) * HD] * factor
        q = q * cosine + pltpu.roll(q, HD // 2, axis=1) * sine
        queries.append(q.astype(BF16))

    head = index // rep
    for kind in range(2):
        for piece in range(pieces):
            g = (kind * half + head * pieces + piece) // units
            for step, to, source in hops:
                dst = kv_dst.at[kind, piece, dp_rows(source)]
                wait = push(dst, dst, sem_kv, (kind * pieces + piece) * size_d + step, {"tensor": tensor})
                if step:
                    wait.wait_recv()
                else:
                    @pl.when(g != index)
                    def _():
                        wait.wait_recv()

    def whole(kind):
        return jnp.concatenate([kv_dst[kind, piece] for piece in range(pieces)], axis=1) if pieces > 1 else kv_dst[kind, 0]

    keys = whole(0).astype(F32)
    keys = (keys * cos_ref[...] + pltpu.roll(keys, HD // 2, axis=1) * sin_ref[...]).astype(BF16)
    values = whole(1)
    total_rows = keys.shape[0]
    shape = (local_rows, total_rows)
    allowed = lax.broadcasted_iota(jnp.int32, shape, 1) <= (
        lax.broadcasted_iota(jnp.int32, shape, 0) + me * local_rows
    )
    for h in range(heads_dev):
        scores = lax.dot_general(
            queries[h], keys, (((1,), (1,)), ((), ())), preferred_element_type=F32
        ) * HD ** (-0.5)
        scores = jnp.where(allowed, scores, -1e30)
        expo = jnp.exp(scores - jnp.max(scores, axis=-1, keepdims=True))
        probs = (expo / jnp.sum(expo, axis=-1, keepdims=True)).astype(BF16)
        att_ref[:, h * HD : (h + 1) * HD] = jnp.dot(
            probs, values, preferred_element_type=F32
        ).astype(BF16)

    def end(copy, i, kind, piece, local):
        if not local:
            copy.wait_send()

    each_send(end)


def front(tokens, gain, cosine, sine, w_query, w_keyval, collective_id):
    size_s, size_t, size_d = lax.axis_size("section"), lax.axis_size("tensor"), lax.axis_size("dp")
    count = size_s * size_t
    local_rows, width = tokens.shape
    kv_cols = w_keyval.shape[1]
    unit = min(kv_cols, HD)
    pieces = HD // unit
    rep = (H // KVH) // (w_query.shape[1] // HD)
    arrivals = 2 * pieces * size_d
    return pl.pallas_call(
        front_body,
        out_shape=(
            jax.ShapeDtypeStruct((local_rows, w_query.shape[1]), BF16),
            jax.ShapeDtypeStruct((local_rows, count * width), BF16),
        ),
        in_specs=[VMEM, VMEM, VMEM, VMEM, ANY, ANY],
        out_specs=(VMEM, VMEM),
        scratch_shapes=[
            pltpu.VMEM((count, local_rows, width), BF16),
            pltpu.VMEM((count, width, w_query.shape[1]), BF16),
            pltpu.VMEM((count, width, kv_cols), BF16),
            pltpu.VMEM((local_rows, w_query.shape[1]), F32),
            pltpu.VMEM((local_rows, kv_cols), F32),
            pltpu.VMEM((local_rows, 1), F32),
            pltpu.VMEM((kv_cols // unit, local_rows, unit), BF16),
            pltpu.VMEM((2, pieces, local_rows * size_d, unit), BF16),
            pltpu.SemaphoreType.DMA((2, count)),
            pltpu.SemaphoreType.DMA,
            dma_sems(size_t - 1),
            dma_sems(size_t * (size_s - 1)),
            dma_sems(arrivals),
            pltpu.SemaphoreType.DMA((kv_cols // unit * rep * size_d,)),
        ],
        compiler_params=pltpu.CompilerParams(
            collective_id=collective_id, has_side_effects=True, vmem_limit_bytes=66000000
        ),
    )(tokens, gain, cosine, sine, w_query, w_keyval)


def tile_of(width, most):
    return width if width <= most else most


def scatter_group(part, pair_rx, comb, z_rx, sem_p, sem_z):
    section, tensor = lax.axis_index("section"), lax.axis_index("tensor")
    size_t = lax.axis_size("tensor")
    block = z_rx.shape[1]

    def rows(s, t):
        return pl.ds(pl.multiple_of((s * size_t + t) * block, block), block)

    sections, tensors = others("section"), others("tensor")
    order = [(step, to) for step, to, _ in tensors] + [(0, tensor)]
    started = []
    for step, to in order:
        for hop, other, _ in sections:
            copy = push(
                part.at[rows(other, to)],
                pair_rx.at[hop - 1, step],
                sem_p,
                (hop - 1) * size_t + step,
                {"section": other},
            )
            copy.start()
            started.append(copy)

    def paired(step, to):
        total = part[rows(section, to), :].astype(F32)
        for hop, other, _ in sections:
            push(
                part.at[rows(other, to)],
                pair_rx.at[hop - 1, step],
                sem_p,
                (hop - 1) * size_t + step,
                {"section": other},
            ).wait_recv()
            total = total + pair_rx[hop - 1, step].astype(F32)
        return total

    for step, to, _ in tensors:
        comb[step - 1] = paired(step, to).astype(BF16)
        copy = push(comb.at[step - 1], z_rx.at[step - 1], sem_z, step - 1, {"tensor": to})
        copy.start()
        started.append(copy)
    total = paired(0, tensor)
    for step, to, _ in tensors:
        push(comb.at[step - 1], z_rx.at[step - 1], sem_z, step - 1, {"tensor": to}).wait_recv()
        total = total + z_rx[step - 1].astype(F32)
    for copy in started:
        copy.wait_send()
    return total


def back_body(
    att_ref, rows_ref, gain_ref, wo_hbm, wg_hbm, wu_hbm, wd_hbm, out_ref,
    wo, wg, wu, wd, att_all, part, pair_rx, comb, z_rx, resid, mid, stat_tx, stat_rx,
    nrm, gu, rx1, tx2, rx2, hid, acc, part2, pair_rx2, comb2, z_rx2,
    sem_w, sem_own, sem_att, sem_res, sem_p, sem_z, sem_stat, sem_t, sem_s,
    sem_1, sem_2, sem_h, sem_p2, sem_z2,
):
    section, tensor, me = lax.axis_index("section"), lax.axis_index("tensor"), lax.axis_index("dp")
    size_t, size_d = lax.axis_size("tensor"), lax.axis_size("dp")
    group_index = section * size_t + tensor
    local_rows, width = att_ref.shape
    block, cols = mid.shape
    total_rows = att_all.shape[0]
    features = rows_ref.shape[1]
    chunks = gu.shape[0]
    dps = others("dp")
    sends = []

    loads = [
        pltpu.make_async_copy(wo_hbm.at[:, pl.ds(pl.multiple_of(me * cols, cols), cols)], wo, sem_w.at[0]),
        pltpu.make_async_copy(wg_hbm, wg, sem_w.at[1]),
        pltpu.make_async_copy(wu_hbm, wu, sem_w.at[2]),
        pltpu.make_async_copy(wd_hbm, wd, sem_w.at[3]),
    ]
    for load in loads:
        load.start()

    greet(group_peers() + [{"dp": to} for _, to, _ in dps])

    def dp_rows(index):
        return pl.ds(pl.multiple_of(index * local_rows, local_rows), local_rows)

    for step, to, _ in dps:
        copy = push(att_ref, att_all.at[dp_rows(me)], sem_att, step - 1, {"dp": to})
        copy.start()
        sends.append(copy)

    per = local_rows // block
    holder = group_index // per
    held_rows = pl.ds(pl.multiple_of(lax.rem(group_index, per) * block, block), block)

    def resid_copy(step, to):
        src = rows_ref.at[held_rows, pl.ds(pl.multiple_of(to * cols, cols), cols)]
        return push(src, resid, sem_res, step - 1, {"dp": to})

    @pl.when(me == holder)
    def _():
        for step, to, _ in dps:
            resid_copy(step, to).start()
        resid[...] = rows_ref[held_rows, pl.ds(pl.multiple_of(me * cols, cols), cols)]

    att_all[dp_rows(me), :] = att_ref[...]
    loads[0].wait()
    tile = tile_of(cols, 512)

    def out_part(index):
        lines = att_all[dp_rows(index), :]

        @pl.loop(0, cols // tile)
        def _(j):
            at = pl.ds(pl.multiple_of(j * tile, tile), tile)
            part[dp_rows(index), at] = jnp.dot(lines, wo[:, at], preferred_element_type=F32).astype(BF16)

    out_part(me)
    for step, to, source in dps:
        push(att_ref, att_all.at[dp_rows(source)], sem_att, step - 1, {"dp": to}).wait_recv()
        out_part(source)

    summed = scatter_group(part, pair_rx, comb, z_rx, sem_p, sem_z)

    for step, to, source in dps:
        @pl.when(source == holder)
        def _():
            resid_copy(step, to).wait_recv()

    @pl.when(me == holder)
    def _():
        for step, to, _ in dps:
            resid_copy(step, to).wait_send()

    mid_rows = (resid[...].astype(F32) + summed).astype(BF16)
    mid[...] = mid_rows
    squares = mid_rows.astype(F32)
    stat = jnp.sum(squares * squares, axis=-1, keepdims=True)
    stat_tx[...] = jnp.broadcast_to(stat, stat_tx.shape)
    for step, to, _ in dps:
        copy = push(stat_tx, stat_rx.at[step - 1], sem_stat, step - 1, {"dp": to})
        copy.start()
        sends.append(copy)
    for step, to, _ in dps:
        push(stat_tx, stat_rx.at[step - 1], sem_stat, step - 1, {"dp": to}).wait_recv()
        stat = stat + stat_rx[step - 1][:, :1]
    factor = lax.rsqrt(stat * (1.0 / features) + EPS)

    def token_rows(s, t):
        return pl.ds(pl.multiple_of((s * size_t + t) * block, block), block)

    nrm[token_rows(section, tensor), :] = (
        mid[...].astype(F32) * factor * gain_ref[...].astype(F32)
    ).astype(BF16)
    gather_group(nrm, token_rows, sem_t, sem_s)

    loads[1].wait()
    loads[2].wait()
    share = gu.shape[2] // 2
    gtile = tile_of(share, 256)
    square = size_d == 4
    if square:
        x, y = lax.rem(me, 2), me // 2
        near = [y * 2 + (1 - x), (1 - y) * 2 + x]
        far = (1 - y) * 2 + (1 - x)
    for c in range(chunks):
        @pl.loop(0, share // gtile)
        def _(j):
            src = pl.ds(pl.multiple_of(c * share + j * gtile, gtile), gtile)
            lo = pl.ds(pl.multiple_of(j * gtile, gtile), gtile)
            hi = pl.ds(pl.multiple_of(share + j * gtile, gtile), gtile)
            gu[c, :, lo] = jnp.dot(nrm[...], wg[:, src], preferred_element_type=F32).astype(BF16)
            gu[c, :, hi] = jnp.dot(nrm[...], wu[:, src], preferred_element_type=F32).astype(BF16)

        if square:
            first = near[c % 2]
            for slot, owner in ((1, far), (0, first)):
                copy = push(gu.at[c, dp_rows(owner)], rx1.at[c, slot], sem_1, 2 * c + slot, {"dp": first})
                copy.start()
                sends.append(copy)
        else:
            for step, to, _ in dps:
                slot = step - 1
                copy = push(gu.at[c, dp_rows(to)], rx1.at[c, slot], sem_1, (size_d - 1) * c + slot, {"dp": to})
                copy.start()
                sends.append(copy)

    if square:
        for c in range(chunks):
            first, second = near[c % 2], near[1 - c % 2]
            push(gu.at[c, dp_rows(far)], rx1.at[c, 1], sem_1, 2 * c + 1, {"dp": first}).wait_recv()
            tx2[c] = (gu[c, dp_rows(second), :].astype(F32) + rx1[c, 1].astype(F32)).astype(BF16)
            copy = push(tx2.at[c], rx2.at[c], sem_2, c, {"dp": second})
            copy.start()
            sends.append(copy)

    hid_slots = size_d - 1
    for c in range(chunks):
        both = gu[c, dp_rows(me), :].astype(F32)
        if square:
            first, second = near[c % 2], near[1 - c % 2]
            push(gu.at[c, dp_rows(first)], rx1.at[c, 0], sem_1, 2 * c, {"dp": first}).wait_recv()
            push(tx2.at[c], rx2.at[c], sem_2, c, {"dp": second}).wait_recv()
            both = both + rx1[c, 0].astype(F32) + rx2[c].astype(F32)
        else:
            for step, to, _ in dps:
                slot = step - 1
                push(
                    gu.at[c, dp_rows(to)], rx1.at[c, slot], sem_1, (size_d - 1) * c + slot, {"dp": to}
                ).wait_recv()
                both = both + rx1[c, slot].astype(F32)
        gate, up = both[:, :share], both[:, share:]
        hid[c, dp_rows(me), :] = (gate / (1.0 + jnp.exp(-gate)) * up).astype(BF16)
        mine = hid.at[c, dp_rows(me)]
        targets = list(enumerate(near)) if square else [(step - 1, to) for step, to, _ in dps]
        for slot, to in targets:
            copy = push(mine, mine, sem_h, hid_slots * c + slot, {"dp": to})
            copy.start()
            sends.append(copy)

    if square:
        for c in range(chunks):
            one, two = c % 2, 1 - c % 2
            theirs = hid.at[c, dp_rows(near[one])]
            push(theirs, theirs, sem_h, hid_slots * c + one, {"dp": near[one]}).wait_recv()
            copy = push(theirs, theirs, sem_h, hid_slots * c + 2, {"dp": near[two]})
            copy.start()
            sends.append(copy)

    loads[3].wait()
    for c in range(chunks):
        if square:
            two = 1 - c % 2
            arrivals = [(two, near[two]), (2, far)]
        else:
            arrivals = [(step - 1, source) for step, _, source in dps]
        for slot, source in arrivals:
            theirs = hid.at[c, dp_rows(source)]
            push(theirs, theirs, sem_h, hid_slots * c + slot, {"dp": source}).wait_recv()

        @pl.loop(0, cols // tile)
        def _(j):
            at = pl.ds(pl.multiple_of(j * tile, tile), tile)
            term = jnp.dot(hid[c], wd[c * share : (c + 1) * share, at], preferred_element_type=F32)
            if c > 0:
                term = acc[:, at] + term
            if c < chunks - 1:
                acc[:, at] = term
            else:
                part2[:, at] = term.astype(BF16)

    total = scatter_group(part2, pair_rx2, comb2, z_rx2, sem_p2, sem_z2)
    out_ref[...] = (mid[...].astype(F32) + total).astype(BF16)
    for copy in sends:
        copy.wait_send()


def back(attended, full_rows, gain, w_out, w_gate, w_up, w_down, collective_id):
    size_s, size_t, size_d = lax.axis_size("section"), lax.axis_size("tensor"), lax.axis_size("dp")
    local_rows, width = attended.shape
    total_rows = local_rows * size_d
    block = total_rows // (size_s * size_t)
    cols, hidden = w_gate.shape
    chunks = min(CHUNKS, hidden // 128)
    share = hidden // chunks
    slots = 2 if size_d == 4 else size_d - 1
    scatter = [
        pltpu.VMEM((total_rows, cols), BF16),
        pltpu.VMEM((size_s - 1, size_t, block, cols), BF16),
        pltpu.VMEM((size_t - 1, block, cols), BF16),
        pltpu.VMEM((size_t - 1, block, cols), BF16),
    ]
    return pl.pallas_call(
        back_body,
        out_shape=jax.ShapeDtypeStruct((block, cols), BF16),
        in_specs=[VMEM, VMEM, VMEM, ANY, ANY, ANY, ANY],
        out_specs=VMEM,
        scratch_shapes=[
            pltpu.VMEM((width, cols), BF16),
            pltpu.VMEM(w_gate.shape, BF16),
            pltpu.VMEM(w_up.shape, BF16),
            pltpu.VMEM(w_down.shape, BF16),
            pltpu.VMEM((total_rows, width), BF16),
            *scatter,
            pltpu.VMEM((block, cols), BF16),
            pltpu.VMEM((block, cols), BF16),
            pltpu.VMEM((block, 128), F32),
            pltpu.VMEM((size_d - 1, block, 128), F32),
            pltpu.VMEM((total_rows, cols), BF16),
            pltpu.VMEM((chunks, total_rows, 2 * share), BF16),
            pltpu.VMEM((chunks, slots, local_rows, 2 * share), BF16),
            pltpu.VMEM((chunks, local_rows, 2 * share), BF16),
            pltpu.VMEM((chunks, local_rows, 2 * share), BF16),
            pltpu.VMEM((chunks, total_rows, share), BF16),
            pltpu.VMEM((total_rows, cols), F32),
            *scatter,
            pltpu.SemaphoreType.DMA((4,)),
            pltpu.SemaphoreType.DMA,
            dma_sems(size_d - 1),
            dma_sems(size_d - 1),
            dma_sems((size_s - 1) * size_t),
            dma_sems(size_t - 1),
            dma_sems(size_d - 1),
            dma_sems(size_t - 1),
            dma_sems(size_t * (size_s - 1)),
            dma_sems(chunks * slots),
            dma_sems(chunks),
            dma_sems(chunks * (size_d - 1)),
            dma_sems((size_s - 1) * size_t),
            dma_sems(size_t - 1),
        ],
        compiler_params=pltpu.CompilerParams(
            collective_id=collective_id, has_side_effects=True, vmem_limit_bytes=66000000
        ),
    )(attended, full_rows, gain, w_out, w_gate, w_up, w_down)


def shards(tokens_in, gain_attn, w_query, w_keyval, w_out, gain_mlp, w_gate, w_up, w_down):
    data_index = lax.axis_index("dp")
    local_rows, width = tokens_in.shape
    total_rows = local_rows * lax.axis_size("dp")
    half_dim = HD // 2
    frequency = THETA ** (-jnp.arange(half_dim, dtype=jnp.float32) * 2.0 / HD)
    angles = jnp.arange(total_rows, dtype=jnp.int32).astype(F32)[:, None] * frequency[None, :]
    cosine, sine = jnp.cos(angles), jnp.sin(angles)
    attended, full_rows = front(
        tokens_in,
        gain_attn.reshape(-1, 1, width),
        jnp.concatenate([cosine, cosine], axis=1),
        jnp.concatenate([-sine, sine], axis=1),
        w_query,
        w_keyval,
        1,
    )
    cols = w_gate.shape[0]
    gain = lax.dynamic_slice_in_dim(gain_mlp, data_index * cols, cols, 0)[None, :]
    return back(attended, full_rows, gain, w_out, w_gate, w_up, w_down, 2)


def solution(mesh):
    placed = (
        P("dp", ("section", "tensor")),
        P(),
        P(None, ("section", "tensor")),
        P(None, ("section", "tensor")),
        P(("section", "tensor"), None),
        P(),
        P("dp", ("section", "tensor")),
        P("dp", ("section", "tensor")),
        P(("section", "tensor"), "dp"),
    )
    return jax.shard_map(
        shards,
        mesh=mesh,
        in_specs=placed,
        out_specs=P(("section", "tensor"), "dp"),
        check_vma=False,
    )
```

profile of v0, /device:TPU:9, one launch (start us, length us, event | category | flops | bytes accessed | tf_op | source)
XLA Modules:
  0.0 213.2 jit_solution(15017062883783523787)
XLA Ops:
  0.0 1.0 fusion
  1.0 1.0 pad_maximum_fusion
  2.0 1.3 reshape.14.gain_ref
  3.4 41.7 %shard_map.91 = (bf16[128,1024]{1,0:T(8,128)(2,1)}, bf16[128,8192]{1,0:T(8,128)(2,1)}) custom-call(bf16[128,1024]{1,0:T(8,128)(2,1)} %x_ref.1, bf16[8,1,1024]{2,1,0:T(2,128)(2,1)} %reshape.14.gain_ref, f32[512,128]{1,0:T(8,128)} %get-tuple-element.12.cos_ref, f32[512,128]{1,0:T(8,128)} %get-tuple-element.13.sin_ref, bf16[8192,1024]{1,0:T(8,128)(2,1)} %wq_hbm.1, ...), custom_call_target="tpu_custom_call" | custom-call | tf_op jit(solution)/shard_map/pallas_call | solution.py:295
  45.1 0.7 dynamic_slice.3
  45.8 0.6 broadcast_in_dim.2.gain_ref
  46.4 165.2 %shard_map.92 = bf16[64,2048]{1,0:T(8,128)(2,1)} custom-call(bf16[128,1024]{1,0:T(8,128)(2,1)} %get-tuple-element.7.att_ref, bf16[128,8192]{1,0:T(8,128)(2,1)} %get-tuple-element.8.rows_ref, bf16[1,2048]{1,0:T(2,128)(2,1)} %broadcast_in_dim.2.gain_ref, bf16[1024,8192]{1,0:T(8,128)(2,1)} %wo_hbm.1, bf16[2048,2048]{1,0:T(8,128)(2,1)} %wg_hbm.1, ...), custom_call_target="tpu_custom_call" | custom-call | tf_op jit(solution)/shard_map/pallas_call | solution.py:597
  211.6 1.7 copy.12
  (2 shorter events, 0.0 us)
where the time goes:
time: 214 us; the launch traced here: 213 us
  Pallas kernels  207 us (97%)
  local copies, waits for them, and re-layouts  4.3 us (2%)
    pallas_call x1, Pallas kernels, back(): pl.pallas_call(back_body, out_shape=jax.ShapeDtypeStruct((block, cols), B...  165 us
    pallas_call x1, Pallas kernels, front(): pl.pallas_call(front_body, out_shape=(jax.ShapeDtypeStruct((local_rows, w...  41.7 us

commit v1 on v0

--- a/solution.py
+++ b/solution.py
@@ -10,7 +10,8 @@
 HD = 128
 EPS = 1e-05
 THETA = 10000.0
-CHUNKS = 8
+CHUNKS = 4
+PARTS = 2
 MESH = pl.DeviceIdType.MESH
 F32 = jnp.float32
 BF16 = jnp.bfloat16
@@ -261,6 +262,8 @@
     keys = (keys * cos_ref[...] + pltpu.roll(keys, HD // 2, axis=1) * sin_ref[...]).astype(BF16)
     values = whole(1)
     total_rows = keys.shape[0]
+    block = total_rows // count
+    sub = block // PARTS
     shape = (local_rows, total_rows)
     allowed = lax.broadcasted_iota(jnp.int32, shape, 1) <= (
         lax.broadcasted_iota(jnp.int32, shape, 0) + me * local_rows
@@ -272,9 +275,10 @@
         scores = jnp.where(allowed, scores, -1e30)
         expo = jnp.exp(scores - jnp.max(scores, axis=-1, keepdims=True))
         probs = (expo / jnp.sum(expo, axis=-1, keepdims=True)).astype(BF16)
-        att_ref[:, h * HD : (h + 1) * HD] = jnp.dot(
-            probs, values, preferred_element_type=F32
-        ).astype(BF16)
+        mixed = jnp.dot(probs, values, preferred_element_type=F32).astype(BF16)
+        for k in range(PARTS):
+            for j in range(local_rows // block):
+                att_ref[k, j * sub : (j + 1) * sub, h * HD : (h + 1) * HD] = mixed[j * block + k * sub :][:sub]
 
     def end(copy, i, kind, piece, local):
         if not local:
@@ -295,7 +299,7 @@
     return pl.pallas_call(
         front_body,
         out_shape=(
-            jax.ShapeDtypeStruct((local_rows, w_query.shape[1]), BF16),
+            jax.ShapeDtypeStruct((PARTS, local_rows // PARTS, w_query.shape[1]), BF16),
             jax.ShapeDtypeStruct((local_rows, count * width), BF16),
         ),
         in_specs=[VMEM, VMEM, VMEM, VMEM, ANY, ANY],
@@ -326,72 +330,24 @@
     return width if width <= most else most
 
 
-def scatter_group(part, pair_rx, comb, z_rx, sem_p, sem_z):
-    section, tensor = lax.axis_index("section"), lax.axis_index("tensor")
-    size_t = lax.axis_size("tensor")
-    block = z_rx.shape[1]
-
-    def rows(s, t):
-        return pl.ds(pl.multiple_of((s * size_t + t) * block, block), block)
-
-    sections, tensors = others("section"), others("tensor")
-    order = [(step, to) for step, to, _ in tensors] + [(0, tensor)]
-    started = []
-    for step, to in order:
-        for hop, other, _ in sections:
-            copy = push(
-                part.at[rows(other, to)],
-                pair_rx.at[hop - 1, step],
-                sem_p,
-                (hop - 1) * size_t + step,
-                {"section": other},
-            )
-            copy.start()
-            started.append(copy)
-
-    def paired(step, to):
-        total = part[rows(section, to), :].astype(F32)
-        for hop, other, _ in sections:
-            push(
-                part.at[rows(other, to)],
-                pair_rx.at[hop - 1, step],
-                sem_p,
-                (hop - 1) * size_t + step,
-                {"section": other},
-            ).wait_recv()
-            total = total + pair_rx[hop - 1, step].astype(F32)
-        return total
-
-    for step, to, _ in tensors:
-        comb[step - 1] = paired(step, to).astype(BF16)
-        copy = push(comb.at[step - 1], z_rx.at[step - 1], sem_z, step - 1, {"tensor": to})
-        copy.start()
-        started.append(copy)
-    total = paired(0, tensor)
-    for step, to, _ in tensors:
-        push(comb.at[step - 1], z_rx.at[step - 1], sem_z, step - 1, {"tensor": to}).wait_recv()
-        total = total + z_rx[step - 1].astype(F32)
-    for copy in started:
-        copy.wait_send()
-    return total
-
-
 def back_body(
     att_ref, rows_ref, gain_ref, wo_hbm, wg_hbm, wu_hbm, wd_hbm, out_ref,
     wo, wg, wu, wd, att_all, part, pair_rx, comb, z_rx, resid, mid, stat_tx, stat_rx,
     nrm, gu, rx1, tx2, rx2, hid, acc, part2, pair_rx2, comb2, z_rx2,
-    sem_w, sem_own, sem_att, sem_res, sem_p, sem_z, sem_stat, sem_t, sem_s,
+    sem_w, sem_att, sem_res, sem_p, sem_z, sem_stat, sem_up, sem_dn, sem_s,
     sem_1, sem_2, sem_h, sem_p2, sem_z2,
 ):
     section, tensor, me = lax.axis_index("section"), lax.axis_index("tensor"), lax.axis_index("dp")
     size_t, size_d = lax.axis_size("tensor"), lax.axis_size("dp")
     group_index = section * size_t + tensor
-    local_rows, width = att_ref.shape
-    block, cols = mid.shape
-    total_rows = att_all.shape[0]
+    parts, dp_sub, width = att_ref.shape
+    local_rows = parts * dp_sub
     features = rows_ref.shape[1]
-    chunks = gu.shape[0]
-    dps = others("dp")
+    _, sub, cols = mid.shape
+    block = parts * sub
+    chunks = gu.shape[1]
+    dps, sections, tensors = others("dp"), others("section"), others("tensor")
+    hops_s = len(sections)
     sends = []
 
     loads = [
@@ -405,13 +361,22 @@
 
     greet(group_peers() + [{"dp": to} for _, to, _ in dps])
 
-    def dp_rows(index):
-        return pl.ds(pl.multiple_of(index * local_rows, local_rows), local_rows)
-
-    for step, to, _ in dps:
-        copy = push(att_ref, att_all.at[dp_rows(me)], sem_att, step - 1, {"dp": to})
+    def send(copy):
         copy.start()
         sends.append(copy)
+
+    def dp_rows(index):
+        return pl.ds(pl.multiple_of(index * dp_sub, dp_sub), dp_sub)
+
+    def group_rows(s, t):
+        return pl.ds(pl.multiple_of((s * size_t + t) * sub, sub), sub)
+
+    def att_copy(k, step, to):
+        return push(att_ref.at[k], att_all.at[k, dp_rows(me)], sem_att, k * (size_d - 1) + step - 1, {"dp": to})
+
+    for k in range(parts):
+        for step, to, _ in dps:
+            send(att_copy(k, step, to))
 
     per = local_rows // block
     holder = group_index // per
@@ -427,176 +392,303 @@
             resid_copy(step, to).start()
         resid[...] = rows_ref[held_rows, pl.ds(pl.multiple_of(me * cols, cols), cols)]
 
-    att_all[dp_rows(me), :] = att_ref[...]
+    for k in range(parts):
+        att_all[k, dp_rows(me), :] = att_ref[k]
     loads[0].wait()
-    tile = tile_of(cols, 512)
-
-    def out_part(index):
-        lines = att_all[dp_rows(index), :]
+    tile = tile_of(cols, 256)
+
+    def pair_copy(k, source, rx, sem, hop, other, step, to):
+        return push(
+            source.at[k, group_rows(other, to)],
+            rx.at[k, hop - 1, step],
+            sem,
+            (k * hops_s + hop - 1) * size_t + step,
+            {"section": other},
+        )
+
+    def pair_start(k, source, rx, sem):
+        for step, to in [(step, to) for step, to, _ in tensors] + [(0, tensor)]:
+            for hop, other, _ in sections:
+                send(pair_copy(k, source, rx, sem, hop, other, step, to))
+
+    def paired(k, source, rx, sem, step, to):
+        total = source[k, group_rows(section, to), :].astype(F32)
+        for hop, other, _ in sections:
+            pair_copy(k, source, rx, sem, hop, other, step, to).wait_recv()
+            total = total + rx[k, hop - 1, step].astype(F32)
+        return total
+
+    def z_copy(k, out, rx, sem, step, to):
+        return push(out.at[k, step - 1], rx.at[k, step - 1], sem, k * (size_t - 1) + step - 1, {"tensor": to})
+
+    def z_start(k, source, rx, sem, out, z_in, sem_out):
+        for step, to, _ in tensors:
+            out[k, step - 1] = paired(k, source, rx, sem, step, to).astype(BF16)
+            send(z_copy(k, out, z_in, sem_out, step, to))
+
+    def z_total(k, source, rx, sem, out, z_in, sem_out):
+        total = paired(k, source, rx, sem, 0, tensor)
+        for step, to, _ in tensors:
+            z_copy(k, out, z_in, sem_out, step, to).wait_recv()
+            total = total + z_in[k, step - 1].astype(F32)
+        return total
+
+    first_set = (part, pair_rx, sem_p)
+    last_set = (part2, pair_rx2, sem_p2)
+
+    def head_out(k):
+        for step, to, _ in dps:
+            att_copy(k, step, to).wait_recv()
 
         @pl.loop(0, cols // tile)
         def _(j):
             at = pl.ds(pl.multiple_of(j * tile, tile), tile)
-            part[dp_rows(index), at] = jnp.dot(lines, wo[:, at], preferred_element_type=F32).astype(BF16)
-
-    out_part(me)
-    for step, to, source in dps:
-        push(att_ref, att_all.at[dp_rows(source)], sem_att, step - 1, {"dp": to}).wait_recv()
-        out_part(source)
-
-    summed = scatter_group(part, pair_rx, comb, z_rx, sem_p, sem_z)
-
-    for step, to, source in dps:
-        @pl.when(source == holder)
+            part[k, :, at] = jnp.dot(att_all[k], wo[:, at], preferred_element_type=F32).astype(BF16)
+
+        pair_start(k, *first_set)
+
+    def head_z(k):
+        z_start(k, *first_set, comb, z_rx, sem_z)
+
+    def up(k, b):
+        at = nrm.at[k, group_rows(section, b)]
+        return push(at, at, sem_up, k * size_t + b, {"tensor": lax.rem(tensor + 1, size_t)})
+
+    def down(k, b):
+        at = nrm.at[k, group_rows(section, b)]
+        return push(at, at, sem_dn, k * size_t + b, {"tensor": lax.rem(tensor + size_t - 1, size_t)})
+
+    def across(k, s, b, hop, other):
+        at = nrm.at[k, group_rows(s, b)]
+        return push(at, at, sem_s, (k * size_t + b) * hops_s + hop - 1, {"section": other})
+
+    def share_block(k, b):
+        for hop, other, _ in sections:
+            across(k, section, b, hop, other).start()
+
+    def middle(k):
+        summed = z_total(k, *first_set, comb, z_rx, sem_z)
+        if k == 0:
+            for step, to, source in dps:
+                @pl.when(source == holder)
+                def _():
+                    resid_copy(step, to).wait_recv()
+
+        rows = (resid[k * sub : (k + 1) * sub].astype(F32) + summed).astype(BF16)
+        mid[k] = rows
+        squares = rows.astype(F32)
+        stat = jnp.sum(squares * squares, axis=-1, keepdims=True)
+        stat_tx[k] = jnp.broadcast_to(stat, stat_tx.shape[1:])
+
+        def stat_copy(step, to):
+            return push(stat_tx.at[k], stat_rx.at[k, step - 1], sem_stat, k * (size_d - 1) + step - 1, {"dp": to})
+
+        for step, to, _ in dps:
+            send(stat_copy(step, to))
+        for step, to, _ in dps:
+            stat_copy(step, to).wait_recv()
+            stat = stat + stat_rx[k, step - 1][:, :1]
+        factor = lax.rsqrt(stat * (1.0 / features) + EPS)
+        nrm[k, group_rows(section, tensor), :] = (
+            mid[k].astype(F32) * factor * gain_ref[...].astype(F32)
+        ).astype(BF16)
+
+        @pl.when(tensor < size_t - 1)
         def _():
-            resid_copy(step, to).wait_recv()
-
-    @pl.when(me == holder)
-    def _():
-        for step, to, _ in dps:
-            resid_copy(step, to).wait_send()
-
-    mid_rows = (resid[...].astype(F32) + summed).astype(BF16)
-    mid[...] = mid_rows
-    squares = mid_rows.astype(F32)
-    stat = jnp.sum(squares * squares, axis=-1, keepdims=True)
-    stat_tx[...] = jnp.broadcast_to(stat, stat_tx.shape)
-    for step, to, _ in dps:
-        copy = push(stat_tx, stat_rx.at[step - 1], sem_stat, step - 1, {"dp": to})
-        copy.start()
-        sends.append(copy)
-    for step, to, _ in dps:
-        push(stat_tx, stat_rx.at[step - 1], sem_stat, step - 1, {"dp": to}).wait_recv()
-        stat = stat + stat_rx[step - 1][:, :1]
-    factor = lax.rsqrt(stat * (1.0 / features) + EPS)
-
-    def token_rows(s, t):
-        return pl.ds(pl.multiple_of((s * size_t + t) * block, block), block)
-
-    nrm[token_rows(section, tensor), :] = (
-        mid[...].astype(F32) * factor * gain_ref[...].astype(F32)
-    ).astype(BF16)
-    gather_group(nrm, token_rows, sem_t, sem_s)
-
-    loads[1].wait()
-    loads[2].wait()
-    share = gu.shape[2] // 2
+            up(k, tensor).start()
+
+        @pl.when(tensor > 0)
+        def _():
+            down(k, tensor).start()
+
+        share_block(k, tensor)
+
+    def relay(k, far):
+        @pl.when(tensor >= far)
+        def _():
+            b = tensor - far
+            up(k, b).wait_recv()
+
+            @pl.when(tensor < size_t - 1)
+            def _():
+                up(k, b).start()
+
+            share_block(k, b)
+
+        @pl.when(tensor + far < size_t)
+        def _():
+            b = tensor + far
+            down(k, b).wait_recv()
+
+            @pl.when(tensor > 0)
+            def _():
+                down(k, b).start()
+
+            share_block(k, b)
+
+    def gathered(k):
+        for b in range(size_t):
+            for hop, other, source in sections:
+                across(k, source, b, hop, other).wait_recv()
+
+    share = gu.shape[3] // 2
     gtile = tile_of(share, 256)
     square = size_d == 4
     if square:
         x, y = lax.rem(me, 2), me // 2
         near = [y * 2 + (1 - x), (1 - y) * 2 + x]
-        far = (1 - y) * 2 + (1 - x)
-    for c in range(chunks):
-        @pl.loop(0, share // gtile)
-        def _(j):
-            src = pl.ds(pl.multiple_of(c * share + j * gtile, gtile), gtile)
-            lo = pl.ds(pl.multiple_of(j * gtile, gtile), gtile)
-            hi = pl.ds(pl.multiple_of(share + j * gtile, gtile), gtile)
-            gu[c, :, lo] = jnp.dot(nrm[...], wg[:, src], preferred_element_type=F32).astype(BF16)
-            gu[c, :, hi] = jnp.dot(nrm[...], wu[:, src], preferred_element_type=F32).astype(BF16)
-
+        far_peer = (1 - y) * 2 + (1 - x)
+    slots = 2 if square else size_d - 1
+    hid_slots = size_d - 1
+
+    def first_copy(k, c, slot, owner, to):
+        return push(
+            gu.at[k, c, dp_rows(owner)], rx1.at[k, c, slot], sem_1, (k * chunks + c) * slots + slot, {"dp": to}
+        )
+
+    def second_copy(k, c, to):
+        return push(tx2.at[k, c], rx2.at[k, c], sem_2, k * chunks + c, {"dp": to})
+
+    def hid_copy(k, c, owner, slot, to):
+        at = hid.at[k, c, dp_rows(owner)]
+        return push(at, at, sem_h, (k * chunks + c) * hid_slots + slot, {"dp": to})
+
+    def gate_up(k):
+        if k == 0:
+            loads[1].wait()
+            loads[2].wait()
+        for c in range(chunks):
+            @pl.loop(0, share // gtile)
+            def _(j):
+                src = pl.ds(pl.multiple_of(c * share + j * gtile, gtile), gtile)
+                lo = pl.ds(pl.multiple_of(j * gtile, gtile), gtile)
+                hi = pl.ds(pl.multiple_of(share + j * gtile, gtile), gtile)
+                gu[k, c, :, lo] = jnp.dot(nrm[k], wg[:, src], preferred_element_type=F32).astype(BF16)
+                gu[k, c, :, hi] = jnp.dot(nrm[k], wu[:, src], preferred_element_type=F32).astype(BF16)
+
+            if square:
+                first = near[c % 2]
+                send(first_copy(k, c, 1, far_peer, first))
+                send(first_copy(k, c, 0, first, first))
+            else:
+                for step, to, _ in dps:
+                    send(first_copy(k, c, step - 1, to, to))
+
+    def second(k, c):
         if square:
-            first = near[c % 2]
-            for slot, owner in ((1, far), (0, first)):
-                copy = push(gu.at[c, dp_rows(owner)], rx1.at[c, slot], sem_1, 2 * c + slot, {"dp": first})
-                copy.start()
-                sends.append(copy)
+            one, two = near[c % 2], near[1 - c % 2]
+            first_copy(k, c, 1, far_peer, one).wait_recv()
+            tx2[k, c] = (gu[k, c, dp_rows(two), :].astype(F32) + rx1[k, c, 1].astype(F32)).astype(BF16)
+            send(second_copy(k, c, two))
+
+    def hidden(k, c):
+        both = gu[k, c, dp_rows(me), :].astype(F32)
+        if square:
+            one, two = near[c % 2], near[1 - c % 2]
+            first_copy(k, c, 0, one, one).wait_recv()
+            second_copy(k, c, two).wait_recv()
+            both = both + rx1[k, c, 0].astype(F32) + rx2[k, c].astype(F32)
         else:
             for step, to, _ in dps:
-                slot = step - 1
-                copy = push(gu.at[c, dp_rows(to)], rx1.at[c, slot], sem_1, (size_d - 1) * c + slot, {"dp": to})
-                copy.start()
-                sends.append(copy)
-
-    if square:
-        for c in range(chunks):
-            first, second = near[c % 2], near[1 - c % 2]
-            push(gu.at[c, dp_rows(far)], rx1.at[c, 1], sem_1, 2 * c + 1, {"dp": first}).wait_recv()
-            tx2[c] = (gu[c, dp_rows(second), :].astype(F32) + rx1[c, 1].astype(F32)).astype(BF16)
-            copy = push(tx2.at[c], rx2.at[c], sem_2, c, {"dp": second})
-            copy.start()
-            sends.append(copy)
-
-    hid_slots = size_d - 1
-    for c in range(chunks):
-        both = gu[c, dp_rows(me), :].astype(F32)
-        if square:
-            first, second = near[c % 2], near[1 - c % 2]
-            push(gu.at[c, dp_rows(first)], rx1.at[c, 0], sem_1, 2 * c, {"dp": first}).wait_recv()
-            push(tx2.at[c], rx2.at[c], sem_2, c, {"dp": second}).wait_recv()
-            both = both + rx1[c, 0].astype(F32) + rx2[c].astype(F32)
-        else:
-            for step, to, _ in dps:
-                slot = step - 1
-                push(
-                    gu.at[c, dp_rows(to)], rx1.at[c, slot], sem_1, (size_d - 1) * c + slot, {"dp": to}
-                ).wait_recv()
-                both = both + rx1[c, slot].astype(F32)
-        gate, up = both[:, :share], both[:, share:]
-        hid[c, dp_rows(me), :] = (gate / (1.0 + jnp.exp(-gate)) * up).astype(BF16)
-        mine = hid.at[c, dp_rows(me)]
+                first_copy(k, c, step - 1, to, to).wait_recv()
+                both = both + rx1[k, c, step - 1].astype(F32)
+        gate, upper = both[:, :share], both[:, share:]
+        hid[k, c, dp_rows(me), :] = (gate / (1.0 + jnp.exp(-gate)) * upper).astype(BF16)
         targets = list(enumerate(near)) if square else [(step - 1, to) for step, to, _ in dps]
         for slot, to in targets:
-            copy = push(mine, mine, sem_h, hid_slots * c + slot, {"dp": to})
-            copy.start()
-            sends.append(copy)
-
-    if square:
-        for c in range(chunks):
+            send(hid_copy(k, c, me, slot, to))
+
+    def pass_hidden(k, c):
+        if square:
             one, two = c % 2, 1 - c % 2
-            theirs = hid.at[c, dp_rows(near[one])]
-            push(theirs, theirs, sem_h, hid_slots * c + one, {"dp": near[one]}).wait_recv()
-            copy = push(theirs, theirs, sem_h, hid_slots * c + 2, {"dp": near[two]})
-            copy.start()
-            sends.append(copy)
-
-    loads[3].wait()
-    for c in range(chunks):
+            hid_copy(k, c, near[one], one, near[one]).wait_recv()
+            send(hid_copy(k, c, near[one], 2, near[two]))
+
+    def down_part(k, c):
+        if k == 0 and c == 0:
+            loads[3].wait()
         if square:
             two = 1 - c % 2
-            arrivals = [(two, near[two]), (2, far)]
+            arrivals = [(two, near[two]), (2, far_peer)]
         else:
             arrivals = [(step - 1, source) for step, _, source in dps]
         for slot, source in arrivals:
-            theirs = hid.at[c, dp_rows(source)]
-            push(theirs, theirs, sem_h, hid_slots * c + slot, {"dp": source}).wait_recv()
+            hid_copy(k, c, source, slot, source).wait_recv()
 
         @pl.loop(0, cols // tile)
         def _(j):
             at = pl.ds(pl.multiple_of(j * tile, tile), tile)
-            term = jnp.dot(hid[c], wd[c * share : (c + 1) * share, at], preferred_element_type=F32)
+            term = jnp.dot(hid[k, c], wd[c * share : (c + 1) * share, at], preferred_element_type=F32)
             if c > 0:
                 term = acc[:, at] + term
             if c < chunks - 1:
                 acc[:, at] = term
             else:
-                part2[:, at] = term.astype(BF16)
-
-    total = scatter_group(part2, pair_rx2, comb2, z_rx2, sem_p2, sem_z2)
-    out_ref[...] = (mid[...].astype(F32) + total).astype(BF16)
+                part2[k, :, at] = term.astype(BF16)
+
+        if c == chunks - 1:
+            pair_start(k, *last_set)
+
+    def down_z(k):
+        z_start(k, *last_set, comb2, z_rx2, sem_z2)
+
+    def finish(k):
+        total = z_total(k, *last_set, comb2, z_rx2, sem_z2)
+        out_ref[k * sub : (k + 1) * sub, :] = (mid[k].astype(F32) + total).astype(BF16)
+
+    def each(act, k):
+        return [(act, k, c) for c in range(chunks)]
+
+    relays = [[(relay, k, far) for far in range(1, size_t)] for k in range(parts)]
+    plan = [(head_out, 0), (head_z, 0)]
+    if parts == 2:
+        plan += [(head_out, 1), (middle, 0), *relays[0][:2], (head_z, 1), *relays[0][2:], (gathered, 0)]
+        plan += [(gate_up, 0), *each(second, 0)[: chunks // 2], (middle, 1), *each(second, 0)[chunks // 2 :]]
+        plan += [*relays[1][:2], *each(hidden, 0), *relays[1][2:], (gathered, 1), (gate_up, 1)]
+        plan += [*each(second, 1), *each(pass_hidden, 0), *each(hidden, 1), *each(down_part, 0), (down_z, 0)]
+        plan += [*each(pass_hidden, 1), *each(down_part, 1), (down_z, 1), (finish, 0), (finish, 1)]
+    for act, *at in plan:
+        act(*at)
+
     for copy in sends:
         copy.wait_send()
+    for k in range(parts):
+        for b in range(size_t):
+            @pl.when((tensor >= b) & (tensor < size_t - 1))
+            def _():
+                up(k, b).wait_send()
+
+            @pl.when((tensor <= b) & (tensor > 0))
+            def _():
+                down(k, b).wait_send()
+
+            for hop, other, _ in sections:
+                across(k, section, b, hop, other).wait_send()
+
+    @pl.when(me == holder)
+    def _():
+        for step, to, _ in dps:
+            resid_copy(step, to).wait_send()
 
 
 def back(attended, full_rows, gain, w_out, w_gate, w_up, w_down, collective_id):
     size_s, size_t, size_d = lax.axis_size("section"), lax.axis_size("tensor"), lax.axis_size("dp")
-    local_rows, width = attended.shape
-    total_rows = local_rows * size_d
-    block = total_rows // (size_s * size_t)
-    cols, hidden = w_gate.shape
-    chunks = min(CHUNKS, hidden // 128)
-    share = hidden // chunks
+    parts, dp_sub, width = attended.shape
+    rows = dp_sub * size_d
+    sub = rows // (size_s * size_t)
+    cols, wide = w_gate.shape
+    chunks = min(CHUNKS, wide // 128)
+    share = wide // chunks
     slots = 2 if size_d == 4 else size_d - 1
     scatter = [
-        pltpu.VMEM((total_rows, cols), BF16),
-        pltpu.VMEM((size_s - 1, size_t, block, cols), BF16),
-        pltpu.VMEM((size_t - 1, block, cols), BF16),
-        pltpu.VMEM((size_t - 1, block, cols), BF16),
+        pltpu.VMEM((parts, rows, cols), BF16),
+        pltpu.VMEM((parts, size_s - 1, size_t, sub, cols), BF16),
+        pltpu.VMEM((parts, size_t - 1, sub, cols), BF16),
+        pltpu.VMEM((parts, size_t - 1, sub, cols), BF16),
     ]
     return pl.pallas_call(
         back_body,
-        out_shape=jax.ShapeDtypeStruct((block, cols), BF16),
+        out_shape=jax.ShapeDtypeStruct((parts * sub, cols), BF16),
         in_specs=[VMEM, VMEM, VMEM, ANY, ANY, ANY, ANY],
         out_specs=VMEM,
         scratch_shapes=[
@@ -604,34 +696,34 @@
             pltpu.VMEM(w_gate.shape, BF16),
             pltpu.VMEM(w_up.shape, BF16),
             pltpu.VMEM(w_down.shape, BF16),
-            pltpu.VMEM((total_rows, width), BF16),
+            pltpu.VMEM((parts, rows, width), BF16),
             *scatter,
-            pltpu.VMEM((block, cols), BF16),
-            pltpu.VMEM((block, cols), BF16),
-            pltpu.VMEM((block, 128), F32),
-            pltpu.VMEM((size_d - 1, block, 128), F32),
-            pltpu.VMEM((total_rows, cols), BF16),
-            pltpu.VMEM((chunks, total_rows, 2 * share), BF16),
-            pltpu.VMEM((chunks, slots, local_rows, 2 * share), BF16),
-            pltpu.VMEM((chunks, local_rows, 2 * share), BF16),
-            pltpu.VMEM((chunks, local_rows, 2 * share), BF16),
-            pltpu.VMEM((chunks, total_rows, share), BF16),
-            pltpu.VMEM((total_rows, cols), F32),
+            pltpu.VMEM((parts * sub, cols), BF16),
+            pltpu.VMEM((parts, sub, cols), BF16),
+            pltpu.VMEM((parts, sub, 128), F32),
+            pltpu.VMEM((parts, size_d - 1, sub, 128), F32),
+            pltpu.VMEM((parts, rows, cols), BF16),
+            pltpu.VMEM((parts, chunks, rows, 2 * share), BF16),
+            pltpu.VMEM((parts, chunks, slots, dp_sub, 2 * share), BF16),
+            pltpu.VMEM((parts, chunks, dp_sub, 2 * share), BF16),
+            pltpu.VMEM((parts, chunks, dp_sub, 2 * share), BF16),
+            pltpu.VMEM((parts, chunks, rows, share), BF16),
+            pltpu.VMEM((rows, cols), F32),
             *scatter,
             pltpu.SemaphoreType.DMA((4,)),
-            pltpu.SemaphoreType.DMA,
+            dma_sems(parts * (size_d - 1)),
             dma_sems(size_d - 1),
-            dma_sems(size_d - 1),
-            dma_sems((size_s - 1) * size_t),
-            dma_sems(size_t - 1),
-            dma_sems(size_d - 1),
-            dma_sems(size_t - 1),
-            dma_sems(size_t * (size_s - 1)),
-            dma_sems(chunks * slots),
-            dma_sems(chunks),
-            dma_sems(chunks * (size_d - 1)),
-            dma_sems((size_s - 1) * size_t),
-            dma_sems(size_t - 1),
+            dma_sems(parts * (size_s - 1) * size_t),
+            dma_sems(parts * (size_t - 1)),
+            dma_sems(parts * (size_d - 1)),
+            dma_sems(parts * size_t),
+            dma_sems(parts * size_t),
+            dma_sems(parts * size_t * (size_s - 1)),
+            dma_sems(parts * chunks * slots),
+            dma_sems(parts * chunks),
+            dma_sems(parts * chunks * (size_d - 1)),
+            dma_sems(parts * (size_s - 1) * size_t),
+            dma_sems(parts * (size_t - 1)),
         ],
         compiler_params=pltpu.CompilerParams(
             collective_id=collective_id, has_side_effects=True, vmem_limit_bytes=66000000

time: 214 us -> 197 us (0.921); the launches traced: 213 us -> 194 us
  Pallas kernels: 207 us -> 187 us
    pallas_call x2, Pallas kernels: 207 us -> 187 us  [the longest x1 146 us: back(): pl.pallas_call(back_body, out_shape=jax.ShapeDtypeStruct((parts * sub, co...]
where the time goes in v1:
time: 197 us; the launch traced here: 194 us
  Pallas kernels  187 us (95%)
  local copies, waits for them, and re-layouts  4.3 us (2%)
  other arithmetic  2.01 us (1%)
    pallas_call x1, Pallas kernels, back(): pl.pallas_call(back_body, out_shape=jax.ShapeDtypeStruct((parts * sub, co...  146 us
    pallas_call x1, Pallas kernels, front(): pl.pallas_call(front_body, out_shape=(jax.ShapeDtypeStruct((PARTS, local_...  41.7 us

profile of v1, /device:TPU:9, one launch (start us, length us, event | category | flops | bytes accessed | tf_op | source)
XLA Modules:
  0.0 193.8 jit_solution(4880492235841258854)
XLA Ops:
  0.0 1.0 fusion
  1.0 1.0 pad_maximum_fusion
  2.0 1.3 reshape.14.gain_ref
  3.4 41.7 %shard_map.91 = (bf16[2,64,1024]{2,1,0:T(8,128)(2,1)}, bf16[128,8192]{1,0:T(8,128)(2,1)}) custom-call(bf16[128,1024]{1,0:T(8,128)(2,1)} %x_ref.1, bf16[8,1,1024]{2,1,0:T(2,128)(2,1)} %reshape.14.gain_ref, f32[512,128]{1,0:T(8,128)} %get-tuple-element.12.cos_ref, f32[512,128]{1,0:T(8,128)} %get-tuple-element.13.sin_ref, bf16[8192,1024]{1,0:T(8,128)(2,1)} %wq_hbm.1, ...), custom_call_target="tpu_custom_call" | custom-call | tf_op jit(solution)/shard_map/pallas_call | solution.py:299
  45.1 0.7 dynamic_slice.3
  45.8 0.6 broadcast_in_dim.2.gain_ref
  46.4 145.7 %shard_map.92 = bf16[64,2048]{1,0:T(8,128)(2,1)} custom-call(bf16[2,64,1024]{2,1,0:T(8,128)(2,1)} %get-tuple-element.7.att_ref, bf16[128,8192]{1,0:T(8,128)(2,1)} %get-tuple-element.8.rows_ref, bf16[1,2048]{1,0:T(2,128)(2,1)} %broadcast_in_dim.2.gain_ref, bf16[1024,8192]{1,0:T(8,128)(2,1)} %wo_hbm.1, bf16[2048,2048]{1,0:T(8,128)(2,1)} %wg_hbm.1, ...), custom_call_target="tpu_custom_call" | custom-call | tf_op jit(solution)/shard_map/pallas_call | solution.py:689
  192.1 1.7 copy.12
  (2 shorter events, 0.0 us)

commit v2 on v1

--- a/solution.py
+++ b/solution.py
@@ -10,8 +10,10 @@
 HD = 128
 EPS = 1e-05
 THETA = 10000.0
-CHUNKS = 4
-PARTS = 2
+CHUNKS = 2
+TILE = 1024
+GTILE = 512
+PIECES = 2
 MESH = pl.DeviceIdType.MESH
 F32 = jnp.float32
 BF16 = jnp.bfloat16
@@ -43,44 +45,61 @@
     return [(step, lax.rem(me + step, size), lax.rem(me + size - step, size)) for step in range(1, size)]
 
 
-def gather_group(out, at, sem_t, sem_s, on_block=lambda section, tensor, order: None):
+def z_routes():
+    tensor, size_t = lax.axis_index("tensor"), lax.axis_size("tensor")
+    if size_t == 4:
+        flip, swap = tensor + 1 - 2 * lax.rem(tensor, 2), lax.rem(tensor + 2, 4)
+        return [(1, swap), (0, flip)], [(0, flip, None), (1, swap, (2, flip)), (2, 3 - tensor, None)]
+    hops = others("tensor")
+    return [(step - 1, to) for step, to, _ in hops], [(step - 1, source, None) for step, _, source in hops]
+
+
+def gather_group(out, sem_t, sem_s, on_block):
     section, tensor = lax.axis_index("section"), lax.axis_index("tensor")
-    sections, tensors = others("section"), others("tensor")
+    sections = others("section")
     size_t = lax.axis_size("tensor")
+    piece = out.shape[1] // PIECES
+    z_sends, z_arrivals = z_routes()
     started = []
 
-    def pass_on(block_t, slot):
-        for step, to, _ in sections:
-            block = out.at[at(section, block_t)]
-            copy = push(block, block, sem_s, slot * len(sections) + step - 1, {"section": to})
-            copy.start()
-            started.append(copy)
-
-    for step, to, _ in tensors:
-        block = out.at[at(section, tensor)]
-        copy = push(block, block, sem_t, step - 1, {"tensor": to})
+    def begin(copy):
         copy.start()
         started.append(copy)
-    pass_on(tensor, 0)
-    on_block(section, tensor, 0)
-
-    def from_sections(slot):
+
+    def z_copy(slot, b, p, to):
+        rows = out.at[section * size_t + b, pl.ds(p * piece, piece)]
+        return push(rows, rows, sem_t, slot * PIECES + p, {"tensor": to})
+
+    def s_copy(slot, s, b, step, to):
+        block = out.at[s * size_t + b]
+        return push(block, block, sem_s, slot * len(sections) + step - 1, {"section": to})
+
+    def pass_on(slot, b):
+        for step, to, _ in sections:
+            begin(s_copy(slot, section, b, step, to))
+
+    for slot, to in z_sends:
+        for p in range(PIECES):
+            begin(z_copy(slot, tensor, p, to))
+    pass_on(size_t - 1, tensor)
+    on_block(section, tensor)
+
+    def from_sections(slot, b):
         for step, to, source in sections:
-            source_t = lax.rem(tensor + size_t - slot, size_t)
-            block = out.at[at(source, source_t)]
-            push(block, block, sem_s, slot * len(sections) + step - 1, {"section": to}).wait_recv()
-            on_block(source, source_t, (slot + 1) * len(sections) + slot + step - 1)
-
-    for step, to, source in tensors:
-        if step == 1:
-            from_sections(0)
-        block = out.at[at(section, source)]
-        push(block, block, sem_t, step - 1, {"tensor": to}).wait_recv()
-        pass_on(source, step)
-        on_block(section, source, step * (len(sections) + 1))
-        if step > 1:
-            from_sections(step - 1)
-    from_sections(size_t - 1)
+            s_copy(slot, source, b, step, to).wait_recv()
+            on_block(source, b)
+
+    late = [(size_t - 1, tensor)]
+    for slot, source, onward in z_arrivals:
+        for p in range(PIECES):
+            z_copy(slot, source, p, source).wait_recv()
+            if onward:
+                begin(z_copy(onward[0], source, p, onward[1]))
+        pass_on(slot, source)
+        from_sections(*late.pop())
+        on_block(section, source)
+        late.append((slot, source))
+    from_sections(*late.pop())
     for copy in started:
         copy.wait_send()
 
@@ -97,17 +116,15 @@
 
 def block_order():
     section, tensor = lax.axis_index("section"), lax.axis_index("tensor")
-    size_t = lax.axis_size("tensor")
-
-    def from_sections(slot):
-        return [(source, lax.rem(tensor + size_t - slot, size_t)) for _, _, source in others("section")]
-
-    order = [(section, tensor)] + from_sections(0)
-    for step, _, source in others("tensor"):
-        order.append((section, source))
-        if step > 1:
-            order += from_sections(step - 1)
-    return order + from_sections(size_t - 1)
+    order, late = [(section, tensor)], tensor
+    for _, b, _ in z_routes()[1]:
+        order += [(source, late) for _, _, source in others("section")] + [(section, b)]
+        late = b
+    return order + [(source, late) for _, _, source in others("section")]
+
+
+def parts_of(block):
+    return max(1, block // 16)
 
 
 def front_body(
@@ -161,7 +178,7 @@
 
     seen = []
 
-    def on_block(s, t, _):
+    def on_block(s, t):
         k = len(seen)
         seen.append(k)
         for load in loads[k]:
@@ -184,7 +201,7 @@
         term = jnp.dot(scaled, wk[k], preferred_element_type=F32)
         kacc[...] = term if k == 0 else kacc[...] + term
 
-    gather_group(blocks, lambda s, t: s * size_t + t, sem_t, sem_s, on_block)
+    gather_group(blocks, sem_t, sem_s, on_block)
     factor = lax.rsqrt(stat[...] * (1.0 / features) + EPS)
 
     for i in range(units):
@@ -263,7 +280,8 @@
     values = whole(1)
     total_rows = keys.shape[0]
     block = total_rows // count
-    sub = block // PARTS
+    parts = parts_of(block)
+    sub = block // parts
     shape = (local_rows, total_rows)
     allowed = lax.broadcasted_iota(jnp.int32, shape, 1) <= (
         lax.broadcasted_iota(jnp.int32, shape, 0) + me * local_rows
@@ -276,7 +294,7 @@
         expo = jnp.exp(scores - jnp.max(scores, axis=-1, keepdims=True))
         probs = (expo / jnp.sum(expo, axis=-1, keepdims=True)).astype(BF16)
         mixed = jnp.dot(probs, values, preferred_element_type=F32).astype(BF16)
-        for k in range(PARTS):
+        for k in range(parts):
             for j in range(local_rows // block):
                 att_ref[k, j * sub : (j + 1) * sub, h * HD : (h + 1) * HD] = mixed[j * block + k * sub :][:sub]
 
@@ -296,10 +314,11 @@
     pieces = HD // unit
     rep = (H // KVH) // (w_query.shape[1] // HD)
     arrivals = 2 * pieces * size_d
+    parts = parts_of(local_rows * size_d // count)
     return pl.pallas_call(
         front_body,
         out_shape=(
-            jax.ShapeDtypeStruct((PARTS, local_rows // PARTS, w_query.shape[1]), BF16),
+            jax.ShapeDtypeStruct((parts, local_rows // parts, w_query.shape[1]), BF16),
             jax.ShapeDtypeStruct((local_rows, count * width), BF16),
         ),
         in_specs=[VMEM, VMEM, VMEM, VMEM, ANY, ANY],
@@ -315,7 +334,7 @@
             pltpu.VMEM((2, pieces, local_rows * size_d, unit), BF16),
             pltpu.SemaphoreType.DMA((2, count)),
             pltpu.SemaphoreType.DMA,
-            dma_sems(size_t - 1),
+            dma_sems((size_t - 1) * PIECES),
             dma_sems(size_t * (size_s - 1)),
             dma_sems(arrivals),
             pltpu.SemaphoreType.DMA((kv_cols // unit * rep * size_d,)),
@@ -332,9 +351,9 @@
 
 def back_body(
     att_ref, rows_ref, gain_ref, wo_hbm, wg_hbm, wu_hbm, wd_hbm, out_ref,
-    wo, wg, wu, wd, att_all, part, pair_rx, comb, z_rx, resid, mid, stat_tx, stat_rx,
-    nrm, gu, rx1, tx2, rx2, hid, acc, part2, pair_rx2, comb2, z_rx2,
-    sem_w, sem_att, sem_res, sem_p, sem_z, sem_stat, sem_up, sem_dn, sem_s,
+    wo, wg, wu, wd, att_all, part, pair_rx, comb, z_rx, resid, stat_tx, stat_rx,
+    nrm, scaled, gu, rx1, tx2, rx2, hid, part2, pair_rx2, comb2, z_rx2,
+    sem_w, sem_att, sem_res, sem_p, sem_z, sem_stat, sem_t, sem_s,
     sem_1, sem_2, sem_h, sem_p2, sem_z2,
 ):
     section, tensor, me = lax.axis_index("section"), lax.axis_index("tensor"), lax.axis_index("dp")
@@ -343,8 +362,8 @@
     parts, dp_sub, width = att_ref.shape
     local_rows = parts * dp_sub
     features = rows_ref.shape[1]
-    _, sub, cols = mid.shape
-    block = parts * sub
+    block, cols = resid.shape
+    sub = block // parts
     chunks = gu.shape[1]
     dps, sections, tensors = others("dp"), others("section"), others("tensor")
     hops_s = len(sections)
@@ -356,8 +375,7 @@
         pltpu.make_async_copy(wu_hbm, wu, sem_w.at[2]),
         pltpu.make_async_copy(wd_hbm, wd, sem_w.at[3]),
     ]
-    for load in loads:
-        load.start()
+    loads[0].start()
 
     greet(group_peers() + [{"dp": to} for _, to, _ in dps])
 
@@ -374,10 +392,12 @@
     def att_copy(k, step, to):
         return push(att_ref.at[k], att_all.at[k, dp_rows(me)], sem_att, k * (size_d - 1) + step - 1, {"dp": to})
 
-    for k in range(parts):
+    def att_start(k):
         for step, to, _ in dps:
-            send(att_copy(k, step, to))
-
+            if k < parts:
+                send(att_copy(k, step, to))
+
+    att_start(0)
     per = local_rows // block
     holder = group_index // per
     held_rows = pl.ds(pl.multiple_of(lax.rem(group_index, per) * block, block), block)
@@ -385,6 +405,11 @@
     def resid_copy(step, to):
         src = rows_ref.at[held_rows, pl.ds(pl.multiple_of(to * cols, cols), cols)]
         return push(src, resid, sem_res, step - 1, {"dp": to})
+
+    loads[0].wait()
+    att_start(1)
+    for load in loads[1:]:
+        load.start()
 
     @pl.when(me == holder)
     def _():
@@ -394,8 +419,7 @@
 
     for k in range(parts):
         att_all[k, dp_rows(me), :] = att_ref[k]
-    loads[0].wait()
-    tile = tile_of(cols, 256)
+    tile = tile_of(cols, TILE)
 
     def pair_copy(k, source, rx, sem, hop, other, step, to):
         return push(
@@ -439,6 +463,7 @@
     def head_out(k):
         for step, to, _ in dps:
             att_copy(k, step, to).wait_recv()
+        att_start(k + 2)
 
         @pl.loop(0, cols // tile)
         def _(j):
@@ -450,21 +475,19 @@
     def head_z(k):
         z_start(k, *first_set, comb, z_rx, sem_z)
 
-    def up(k, b):
+    z_sends, z_arrivals = z_routes()
+
+    def pass_copy(k, slot, b, to):
         at = nrm.at[k, group_rows(section, b)]
-        return push(at, at, sem_up, k * size_t + b, {"tensor": lax.rem(tensor + 1, size_t)})
-
-    def down(k, b):
-        at = nrm.at[k, group_rows(section, b)]
-        return push(at, at, sem_dn, k * size_t + b, {"tensor": lax.rem(tensor + size_t - 1, size_t)})
-
-    def across(k, s, b, hop, other):
+        return push(at, at, sem_t, k * (size_t - 1) + slot, {"tensor": to})
+
+    def across(k, s, b, slot, hop, other):
         at = nrm.at[k, group_rows(s, b)]
-        return push(at, at, sem_s, (k * size_t + b) * hops_s + hop - 1, {"section": other})
-
-    def share_block(k, b):
+        return push(at, at, sem_s, (k * size_t + slot) * hops_s + hop - 1, {"section": other})
+
+    def share_block(k, b, slot):
         for hop, other, _ in sections:
-            across(k, section, b, hop, other).start()
+            send(across(k, section, b, slot, hop, other))
 
     def middle(k):
         summed = z_total(k, *first_set, comb, z_rx, sem_z)
@@ -475,64 +498,53 @@
                     resid_copy(step, to).wait_recv()
 
         rows = (resid[k * sub : (k + 1) * sub].astype(F32) + summed).astype(BF16)
-        mid[k] = rows
-        squares = rows.astype(F32)
-        stat = jnp.sum(squares * squares, axis=-1, keepdims=True)
-        stat_tx[k] = jnp.broadcast_to(stat, stat_tx.shape[1:])
-
-        def stat_copy(step, to):
-            return push(stat_tx.at[k], stat_rx.at[k, step - 1], sem_stat, k * (size_d - 1) + step - 1, {"dp": to})
+        nrm[k, group_rows(section, tensor), :] = rows
+        for slot, to in z_sends:
+            send(pass_copy(k, slot, tensor, to))
+        share_block(k, tensor, size_t - 1)
+
+    def relay(k):
+        for slot, source, onward in z_arrivals:
+            pass_copy(k, slot, source, source).wait_recv()
+            if onward:
+                send(pass_copy(k, onward[0], source, onward[1]))
+            share_block(k, source, slot)
+
+    def gathered(k):
+        for slot, b in [(size_t - 1, tensor)] + [(slot, source) for slot, source, _ in z_arrivals]:
+            for hop, other, source in sections:
+                across(k, source, b, slot, hop, other).wait_recv()
+
+    def stat_copy(k, step, to):
+        return push(
+            stat_tx.at[k, dp_rows(to)], stat_rx.at[k, step - 1], sem_stat, k * (size_d - 1) + step - 1, {"dp": to}
+        )
+
+    def scale(k):
+        @pl.loop(0, stat_tx.shape[1] // 16)
+        def _(j):
+            at = pl.ds(pl.multiple_of(j * 16, 16), 16)
+            rows = nrm[k, at, :].astype(F32)
+            stat = jnp.sum(rows * rows, axis=-1, keepdims=True)
+            stat_tx[k, at, :] = jnp.broadcast_to(stat, (16, 128))
+            scaled[at, :] = (rows * gain_ref[...].astype(F32)).astype(BF16)
 
         for step, to, _ in dps:
-            send(stat_copy(step, to))
-        for step, to, _ in dps:
-            stat_copy(step, to).wait_recv()
-            stat = stat + stat_rx[k, step - 1][:, :1]
-        factor = lax.rsqrt(stat * (1.0 / features) + EPS)
-        nrm[k, group_rows(section, tensor), :] = (
-            mid[k].astype(F32) * factor * gain_ref[...].astype(F32)
-        ).astype(BF16)
-
-        @pl.when(tensor < size_t - 1)
-        def _():
-            up(k, tensor).start()
-
-        @pl.when(tensor > 0)
-        def _():
-            down(k, tensor).start()
-
-        share_block(k, tensor)
-
-    def relay(k, far):
-        @pl.when(tensor >= far)
-        def _():
-            b = tensor - far
-            up(k, b).wait_recv()
-
-            @pl.when(tensor < size_t - 1)
-            def _():
-                up(k, b).start()
-
-            share_block(k, b)
-
-        @pl.when(tensor + far < size_t)
-        def _():
-            b = tensor + far
-            down(k, b).wait_recv()
-
-            @pl.when(tensor > 0)
-            def _():
-                down(k, b).start()
-
-            share_block(k, b)
-
-    def gathered(k):
-        for b in range(size_t):
-            for hop, other, source in sections:
-                across(k, source, b, hop, other).wait_recv()
+            send(stat_copy(k, step, to))
+
+    factors = {}
+
+    def factor_of(k):
+        if k not in factors:
+            stat = stat_tx[k, dp_rows(me), :][:, :1]
+            for step, to, _ in dps:
+                stat_copy(k, step, to).wait_recv()
+                stat = stat + stat_rx[k, step - 1][:, :1]
+            factors[k] = lax.rsqrt(stat * (1.0 / features) + EPS)
+        return factors[k]
 
     share = gu.shape[3] // 2
-    gtile = tile_of(share, 256)
+    gtile = tile_of(share, GTILE)
     square = size_d == 4
     if square:
         x, y = lax.rem(me, 2), me // 2
@@ -557,14 +569,15 @@
         if k == 0:
             loads[1].wait()
             loads[2].wait()
+        scale(k)
         for c in range(chunks):
             @pl.loop(0, share // gtile)
             def _(j):
                 src = pl.ds(pl.multiple_of(c * share + j * gtile, gtile), gtile)
                 lo = pl.ds(pl.multiple_of(j * gtile, gtile), gtile)
                 hi = pl.ds(pl.multiple_of(share + j * gtile, gtile), gtile)
-                gu[k, c, :, lo] = jnp.dot(nrm[k], wg[:, src], preferred_element_type=F32).astype(BF16)
-                gu[k, c, :, hi] = jnp.dot(nrm[k], wu[:, src], preferred_element_type=F32).astype(BF16)
+                gu[k, c, :, lo] = jnp.dot(scaled[...], wg[:, src], preferred_element_type=F32).astype(BF16)
+                gu[k, c, :, hi] = jnp.dot(scaled[...], wu[:, src], preferred_element_type=F32).astype(BF16)
 
             if square:
                 first = near[c % 2]
@@ -592,6 +605,7 @@
             for step, to, _ in dps:
                 first_copy(k, c, step - 1, to, to).wait_recv()
                 both = both + rx1[k, c, step - 1].astype(F32)
+        both = both * factor_of(k)
         gate, upper = both[:, :share], both[:, share:]
         hid[k, c, dp_rows(me), :] = (gate / (1.0 + jnp.exp(-gate)) * upper).astype(BF16)
         targets = list(enumerate(near)) if square else [(step - 1, to) for step, to, _ in dps]
@@ -604,7 +618,7 @@
             hid_copy(k, c, near[one], one, near[one]).wait_recv()
             send(hid_copy(k, c, near[one], 2, near[two]))
 
-    def down_part(k, c):
+    def down_wait(k, c):
         if k == 0 and c == 0:
             loads[3].wait()
         if square:
@@ -615,56 +629,62 @@
         for slot, source in arrivals:
             hid_copy(k, c, source, slot, source).wait_recv()
 
+    def down_out(k):
         @pl.loop(0, cols // tile)
         def _(j):
             at = pl.ds(pl.multiple_of(j * tile, tile), tile)
-            term = jnp.dot(hid[k, c], wd[c * share : (c + 1) * share, at], preferred_element_type=F32)
-            if c > 0:
-                term = acc[:, at] + term
-            if c < chunks - 1:
-                acc[:, at] = term
-            else:
-                part2[k, :, at] = term.astype(BF16)
-
-        if c == chunks - 1:
-            pair_start(k, *last_set)
+            term = jnp.dot(hid[k, 0], wd[:share, at], preferred_element_type=F32)
+            for c in range(1, chunks):
+                term = term + jnp.dot(hid[k, c], wd[c * share : (c + 1) * share, at], preferred_element_type=F32)
+            part2[k, :, at] = term.astype(BF16)
+
+        pair_start(k, *last_set)
 
     def down_z(k):
         z_start(k, *last_set, comb2, z_rx2, sem_z2)
 
     def finish(k):
         total = z_total(k, *last_set, comb2, z_rx2, sem_z2)
-        out_ref[k * sub : (k + 1) * sub, :] = (mid[k].astype(F32) + total).astype(BF16)
+        out_ref[k * sub : (k + 1) * sub, :] = (nrm[k, group_rows(section, tensor), :].astype(F32) + total).astype(BF16)
 
     def each(act, k):
         return [(act, k, c) for c in range(chunks)]
 
-    relays = [[(relay, k, far) for far in range(1, size_t)] for k in range(parts)]
     plan = [(head_out, 0), (head_z, 0)]
-    if parts == 2:
-        plan += [(head_out, 1), (middle, 0), *relays[0][:2], (head_z, 1), *relays[0][2:], (gathered, 0)]
-        plan += [(gate_up, 0), *each(second, 0)[: chunks // 2], (middle, 1), *each(second, 0)[chunks // 2 :]]
-        plan += [*relays[1][:2], *each(hidden, 0), *relays[1][2:], (gathered, 1), (gate_up, 1)]
-        plan += [*each(second, 1), *each(pass_hidden, 0), *each(hidden, 1), *each(down_part, 0), (down_z, 0)]
-        plan += [*each(pass_hidden, 1), *each(down_part, 1), (down_z, 1), (finish, 0), (finish, 1)]
+    if parts > 1:
+        plan += [(head_out, 1), (head_z, 1)]
+    plan += [(middle, 0)]
+    if parts > 2:
+        plan += [(head_out, 2)]
+    plan += [(relay, 0), (gathered, 0)]
+    for k in range(parts):
+        if k + 1 < parts:
+            plan += [(middle, k + 1)]
+        if k + 2 < parts:
+            plan += [(head_z, k + 2)]
+        plan += [(gate_up, k)]
+        if k > 0:
+            plan += [*each(pass_hidden, k - 1)]
+        if k + 1 < parts:
+            plan += [(relay, k + 1)]
+        if k + 3 < parts:
+            plan += [(head_out, k + 3)]
+        plan += [*each(second, k)]
+        if k > 0:
+            plan += [*each(down_wait, k - 1), (down_out, k - 1), (down_z, k - 1)]
+        plan += [*each(hidden, k)]
+        if k > 1:
+            plan += [(finish, k - 2)]
+        if k + 1 < parts:
+            plan += [(gathered, k + 1)]
+    last = parts - 1
+    plan += [*each(pass_hidden, last), *each(down_wait, last), (down_out, last), (down_z, last)]
+    plan += [(finish, k) for k in range(max(0, parts - 2), parts)]
     for act, *at in plan:
         act(*at)
 
     for copy in sends:
         copy.wait_send()
-    for k in range(parts):
-        for b in range(size_t):
-            @pl.when((tensor >= b) & (tensor < size_t - 1))
-            def _():
-                up(k, b).wait_send()
-
-            @pl.when((tensor <= b) & (tensor > 0))
-            def _():
-                down(k, b).wait_send()
-
-            for hop, other, _ in sections:
-                across(k, section, b, hop, other).wait_send()
-
     @pl.when(me == holder)
     def _():
         for step, to, _ in dps:
@@ -699,16 +719,15 @@
             pltpu.VMEM((parts, rows, width), BF16),
             *scatter,
             pltpu.VMEM((parts * sub, cols), BF16),
-            pltpu.VMEM((parts, sub, cols), BF16),
-            pltpu.VMEM((parts, sub, 128), F32),
-            pltpu.VMEM((parts, size_d - 1, sub, 128), F32),
+            pltpu.VMEM((parts, rows, 128), F32),
+            pltpu.VMEM((parts, size_d - 1, dp_sub, 128), F32),
             pltpu.VMEM((parts, rows, cols), BF16),
+            pltpu.VMEM((rows, cols), BF16),
             pltpu.VMEM((parts, chunks, rows, 2 * share), BF16),
             pltpu.VMEM((parts, chunks, slots, dp_sub, 2 * share), BF16),
             pltpu.VMEM((parts, chunks, dp_sub, 2 * share), BF16),
             pltpu.VMEM((parts, chunks, dp_sub, 2 * share), BF16),
             pltpu.VMEM((parts, chunks, rows, share), BF16),
-            pltpu.VMEM((rows, cols), F32),
             *scatter,
             pltpu.SemaphoreType.DMA((4,)),
             dma_sems(parts * (size_d - 1)),
@@ -716,8 +735,7 @@
             dma_sems(parts * (size_s - 1) * size_t),
             dma_sems(parts * (size_t - 1)),
             dma_sems(parts * (size_d - 1)),
-            dma_sems(parts * size_t),
-            dma_sems(parts * size_t),
+            dma_sems(parts * (size_t - 1)),
             dma_sems(parts * size_t * (size_s - 1)),
             dma_sems(parts * chunks * slots),
             dma_sems(parts * chunks),

time: 197 us -> 170 us (0.86)
  Pallas kernels: 187 us -> 162 us
    pallas_call x1, Pallas kernels: 146 us -> 122 us  [back(): pl.pallas_call(back_body, out_shape=jax.ShapeDtypeStruct((parts * sub, co...]
where the time goes in v2:
time: 170 us; the launch traced here: 169 us
  Pallas kernels  162 us (95%)
  local copies, waits for them, and re-layouts  4.3 us (3%)
  other arithmetic  2.01 us (1%)
    pallas_call x1, Pallas kernels, back(): pl.pallas_call(back_body, out_shape=jax.ShapeDtypeStruct((parts * sub, co...  122 us
    pallas_call x1, Pallas kernels, front(): pl.pallas_call(front_body, out_shape=(jax.ShapeDtypeStruct((parts, local_...  40.4 us

profile of v2, /device:TPU:9, one launch (start us, length us, event | category | flops | bytes accessed | tf_op | source)
XLA Modules:
  0.0 168.6 jit_solution(14727215751273905266)
XLA Ops:
  0.0 1.0 fusion
  1.0 1.0 pad_maximum_fusion
  2.0 1.3 reshape.14.gain_ref
  3.4 40.4 %shard_map.91 = (bf16[4,32,1024]{2,1,0:T(8,128)(2,1)}, bf16[128,8192]{1,0:T(8,128)(2,1)}) custom-call(bf16[128,1024]{1,0:T(8,128)(2,1)} %x_ref.1, bf16[8,1,1024]{2,1,0:T(2,128)(2,1)} %reshape.14.gain_ref, f32[512,128]{1,0:T(8,128)} %get-tuple-element.12.cos_ref, f32[512,128]{1,0:T(8,128)} %get-tuple-element.13.sin_ref, bf16[8192,1024]{1,0:T(8,128)(2,1)} %wq_hbm.1, ...), custom_call_target="tpu_custom_call" | custom-call | tf_op jit(solution)/shard_map/pallas_call | solution.py:318
  43.8 0.7 dynamic_slice.3
  44.5 0.6 broadcast_in_dim.2.gain_ref
  45.1 121.8 %shard_map.92 = bf16[64,2048]{1,0:T(8,128)(2,1)} custom-call(bf16[4,32,1024]{2,1,0:T(8,128)(2,1)} %get-tuple-element.7.att_ref, bf16[128,8192]{1,0:T(8,128)(2,1)} %get-tuple-element.8.rows_ref, bf16[1,2048]{1,0:T(2,128)(2,1)} %broadcast_in_dim.2.gain_ref, bf16[1024,8192]{1,0:T(8,128)(2,1)} %wo_hbm.1, bf16[2048,2048]{1,0:T(8,128)(2,1)} %wg_hbm.1, ...), custom_call_target="tpu_custom_call" | custom-call | tf_op jit(solution)/shard_map/pallas_call | solution.py:709
  166.9 1.7 copy.12
  (2 shorter events, 0.0 us)

commit v3 on v2

--- a/solution.py
+++ b/solution.py
@@ -1,5 +1,6 @@
 import jax
 import jax.numpy as jnp
+import numpy as np
 from jax import lax
 from jax.experimental import pallas as pl
 from jax.experimental.pallas import tpu as pltpu
@@ -14,6 +15,21 @@
 TILE = 1024
 GTILE = 512
 PIECES = 2
+ORDER = (
+    "H0 Z0 H1 Z1",
+    "M0 H2 M1 R0",
+    "G0 Z2 U0 H3",
+    "R1 G1 Z3 U1",
+    "S0 M2 M3 S1",
+    "R2 G2 U2 D0",
+    "R3 G3 U3 D1",
+    "S2 P0 S3 D2",
+    "P1 D3 V0 W0",
+    "Y0 P2 V1 W1",
+    "Y1 P3 F0 V2",
+    "W2 Y2 F1 V3",
+    "W3 Y3 F2 F3",
+)
 MESH = pl.DeviceIdType.MESH
 F32 = jnp.float32
 BF16 = jnp.bfloat16
@@ -46,10 +62,6 @@
 
 
 def z_routes():
-    tensor, size_t = lax.axis_index("tensor"), lax.axis_size("tensor")
-    if size_t == 4:
-        flip, swap = tensor + 1 - 2 * lax.rem(tensor, 2), lax.rem(tensor + 2, 4)
-        return [(1, swap), (0, flip)], [(0, flip, None), (1, swap, (2, flip)), (2, 3 - tensor, None)]
     hops = others("tensor")
     return [(step - 1, to) for step, to, _ in hops], [(step - 1, source, None) for step, _, source in hops]
 
@@ -59,16 +71,23 @@
     sections = others("section")
     size_t = lax.axis_size("tensor")
     piece = out.shape[1] // PIECES
-    z_sends, z_arrivals = z_routes()
+    line = size_t == 4
     started = []
 
     def begin(copy):
         copy.start()
         started.append(copy)
 
-    def z_copy(slot, b, p, to):
+    def z_copy(b, p, to, slot):
         rows = out.at[section * size_t + b, pl.ds(p * piece, piece)]
-        return push(rows, rows, sem_t, slot * PIECES + p, {"tensor": to})
+        return pltpu.make_async_remote_copy(
+            src_ref=rows,
+            dst_ref=rows,
+            send_sem=sem_t.at[0, slot * PIECES + p],
+            recv_sem=sem_t.at[1, (b if line else slot) * PIECES + p],
+            device_id={"tensor": to},
+            device_id_type=MESH,
+        )
 
     def s_copy(slot, s, b, step, to):
         block = out.at[s * size_t + b]
@@ -77,31 +96,70 @@
     def pass_on(slot, b):
         for step, to, _ in sections:
             begin(s_copy(slot, section, b, step, to))
-
-    for slot, to in z_sends:
-        for p in range(PIECES):
-            begin(z_copy(slot, tensor, p, to))
-    pass_on(size_t - 1, tensor)
-    on_block(section, tensor)
 
     def from_sections(slot, b):
         for step, to, source in sections:
             s_copy(slot, source, b, step, to).wait_recv()
             on_block(source, b)
 
-    late = [(size_t - 1, tensor)]
-    for slot, source, onward in z_arrivals:
+    above, below = lax.rem(tensor + 1, size_t), lax.rem(tensor + size_t - 1, size_t)
+
+    def line_up(p, b, act):
+        @pl.when((b <= tensor) & (tensor < size_t - 1))
+        def _():
+            act(z_copy(b, p, above, b))
+
+    def line_down(p, b, slot, act):
+        @pl.when((b >= tensor) & (tensor > 0))
+        def _():
+            act(z_copy(b, p, below, slot))
+
+    def start(copy):
+        copy.start()
+
+    def done(copy):
+        copy.wait_send()
+
+    sources = near_first()
+    for p in range(PIECES):
+        if line:
+            line_up(p, tensor, start)
+            line_down(p, tensor, size_t, start)
+        else:
+            for step, to, _ in others("tensor"):
+                begin(z_copy(tensor, p, to, step - 1))
+    pass_on(size_t - 1, tensor)
+    on_block(section, tensor)
+    from_sections(size_t - 1, tensor)
+
+    def arrive(slot, p):
+        source = sources[slot]
+        z_copy(source, p, source, slot).wait_recv()
+        if line:
+            line_up(p, source, start)
+            line_down(p, source, source, start)
+        if p == PIECES - 1:
+            pass_on(slot, source)
+
+    for slot, source in enumerate(sources):
         for p in range(PIECES):
-            z_copy(slot, source, p, source).wait_recv()
-            if onward:
-                begin(z_copy(onward[0], source, p, onward[1]))
-        pass_on(slot, source)
-        from_sections(*late.pop())
-        on_block(section, source)
-        late.append((slot, source))
-    from_sections(*late.pop())
+            arrive(slot, p)
+            if slot > 0 and p == 0:
+                on_block(section, sources[slot - 1])
+        if slot > 0:
+            from_sections(slot - 1, sources[slot - 1])
+    last = len(sources) - 1
+    on_block(section, sources[last])
+    from_sections(last, sources[last])
     for copy in started:
         copy.wait_send()
+    if line:
+        for p in range(PIECES):
+            line_down(p, tensor, size_t, done)
+            for b in [tensor, *sources]:
+                line_up(p, b, done)
+            for b in sources:
+                line_down(p, b, b, done)
 
 
 def group_peers():
@@ -114,22 +172,36 @@
     return pltpu.SemaphoreType.DMA((2, max(1, count)))
 
 
+def near_first():
+    tensor = lax.axis_index("tensor")
+    if lax.axis_size("tensor") == 4:
+        upper = tensor // 2
+        return [tensor + 1 - 2 * lax.rem(tensor, 2), 2 - upper, 3 - 3 * upper]
+    return [source for _, _, source in others("tensor")]
+
+
 def block_order():
     section, tensor = lax.axis_index("section"), lax.axis_index("tensor")
-    order, late = [(section, tensor)], tensor
-    for _, b, _ in z_routes()[1]:
-        order += [(source, late) for _, _, source in others("section")] + [(section, b)]
-        late = b
-    return order + [(source, late) for _, _, source in others("section")]
+    order = []
+    for b in [tensor, *near_first()]:
+        order += [(section, b)] + [(source, b) for _, _, source in others("section")]
+    return order
 
 
 def parts_of(block):
     return max(1, block // 16)
 
 
+def times_gain(rows, gain32, first):
+    tiles = range(rows.shape[1] // 128)
+    return jnp.concatenate(
+        [rows[:, i * 128 : (i + 1) * 128] * gain32[pl.ds(first + i, 1), :] for i in tiles], axis=1
+    )
+
+
 def front_body(
     x_ref, gain_ref, cos_ref, sin_ref, wq_hbm, wk_hbm, att_ref, full_ref,
-    blocks, wq, wk, qacc, kacc, stat, kv_src, kv_dst,
+    gain32, blocks, wq, wk, qacc, kacc, stat, kv_src, kv_dst,
     sem_w, sem_own, sem_t, sem_s, sem_kv, sem_kv_out,
 ):
     section, tensor, me = lax.axis_index("section"), lax.axis_index("tensor"), lax.axis_index("dp")
@@ -159,6 +231,7 @@
             load.start()
     own = pltpu.make_async_copy(x_ref, blocks.at[index], sem_own)
     own.start()
+    gain32[...] = gain_ref[...].astype(F32)
 
     dps = others("dp")
     everyone = []
@@ -189,8 +262,8 @@
         rows = raw.astype(F32)
         part = jnp.sum(rows * rows, axis=-1, keepdims=True)
         stat[...] = part if k == 0 else stat[...] + part
-        scaled = (rows * gain_ref[at].astype(F32)).astype(BF16)
-        tile = tile_of(qacc.shape[1], 256)
+        scaled = times_gain(rows, gain32, at * (width // 128)).astype(BF16)
+        tile = tile_of(qacc.shape[1], GTILE)
 
         @pl.loop(0, qacc.shape[1] // tile)
         def _(j):
@@ -324,6 +397,7 @@
         in_specs=[VMEM, VMEM, VMEM, VMEM, ANY, ANY],
         out_specs=(VMEM, VMEM),
         scratch_shapes=[
+            pltpu.VMEM(gain.shape, F32),
             pltpu.VMEM((count, local_rows, width), BF16),
             pltpu.VMEM((count, width, w_query.shape[1]), BF16),
             pltpu.VMEM((count, width, kv_cols), BF16),
@@ -334,7 +408,7 @@
             pltpu.VMEM((2, pieces, local_rows * size_d, unit), BF16),
             pltpu.SemaphoreType.DMA((2, count)),
             pltpu.SemaphoreType.DMA,
-            dma_sems((size_t - 1) * PIECES),
+            dma_sems((size_t + 1) * PIECES),
             dma_sems(size_t * (size_s - 1)),
             dma_sems(arrivals),
             pltpu.SemaphoreType.DMA((kv_cols // unit * rep * size_d,)),
@@ -351,7 +425,7 @@
 
 def back_body(
     att_ref, rows_ref, gain_ref, wo_hbm, wg_hbm, wu_hbm, wd_hbm, out_ref,
-    wo, wg, wu, wd, att_all, part, pair_rx, comb, z_rx, resid, stat_tx, stat_rx,
+    gain32, wo, wg, wu, wd, att_all, part, pair_rx, comb, z_rx, resid, stat_tx, stat_rx,
     nrm, scaled, gu, rx1, tx2, rx2, hid, part2, pair_rx2, comb2, z_rx2,
     sem_w, sem_att, sem_res, sem_p, sem_z, sem_stat, sem_t, sem_s,
     sem_1, sem_2, sem_h, sem_p2, sem_z2,
@@ -376,6 +450,7 @@
         pltpu.make_async_copy(wd_hbm, wd, sem_w.at[3]),
     ]
     loads[0].start()
+    gain32[...] = gain_ref[...].astype(F32)
 
     greet(group_peers() + [{"dp": to} for _, to, _ in dps])
 
@@ -527,7 +602,7 @@
             rows = nrm[k, at, :].astype(F32)
             stat = jnp.sum(rows * rows, axis=-1, keepdims=True)
             stat_tx[k, at, :] = jnp.broadcast_to(stat, (16, 128))
-            scaled[at, :] = (rows * gain_ref[...].astype(F32)).astype(BF16)
+            scaled[at, :] = times_gain(rows, gain32, me * (cols // 128)).astype(BF16)
 
         for step, to, _ in dps:
             send(stat_copy(k, step, to))
@@ -650,36 +725,22 @@
     def each(act, k):
         return [(act, k, c) for c in range(chunks)]
 
-    plan = [(head_out, 0), (head_z, 0)]
-    if parts > 1:
-        plan += [(head_out, 1), (head_z, 1)]
-    plan += [(middle, 0)]
-    if parts > 2:
-        plan += [(head_out, 2)]
-    plan += [(relay, 0), (gathered, 0)]
+    def add(act, k):
+        if 0 <= k < parts and (act, k) not in added:
+            added.append((act, k))
+            plan.extend(each(act, k) if act in (second, hidden, pass_hidden, down_wait) else [(act, k)])
+
+    added, plan = [], []
+    names = {
+        "H": head_out, "Z": head_z, "M": middle, "R": relay, "G": gathered, "U": gate_up, "S": second,
+        "D": hidden, "P": pass_hidden, "V": down_wait, "W": down_out, "Y": down_z, "F": finish,
+    }
+    for line in ORDER:
+        for step in line.split():
+            add(names[step[0]], int(step[1]))
     for k in range(parts):
-        if k + 1 < parts:
-            plan += [(middle, k + 1)]
-        if k + 2 < parts:
-            plan += [(head_z, k + 2)]
-        plan += [(gate_up, k)]
-        if k > 0:
-            plan += [*each(pass_hidden, k - 1)]
-        if k + 1 < parts:
-            plan += [(relay, k + 1)]
-        if k + 3 < parts:
-            plan += [(head_out, k + 3)]
-        plan += [*each(second, k)]
-        if k > 0:
-            plan += [*each(down_wait, k - 1), (down_out, k - 1), (down_z, k - 1)]
-        plan += [*each(hidden, k)]
-        if k > 1:
-            plan += [(finish, k - 2)]
-        if k + 1 < parts:
-            plan += [(gathered, k + 1)]
-    last = parts - 1
-    plan += [*each(pass_hidden, last), *each(down_wait, last), (down_out, last), (down_z, last)]
-    plan += [(finish, k) for k in range(max(0, parts - 2), parts)]
+        for act in names.values():
+            add(act, k)
     for act, *at in plan:
         act(*at)
 
@@ -712,6 +773,7 @@
         in_specs=[VMEM, VMEM, VMEM, ANY, ANY, ANY, ANY],
         out_specs=VMEM,
         scratch_shapes=[
+            pltpu.VMEM(gain.shape, F32),
             pltpu.VMEM((width, cols), BF16),
             pltpu.VMEM(w_gate.shape, BF16),
             pltpu.VMEM(w_up.shape, BF16),
@@ -750,25 +812,21 @@
 
 
 def shards(tokens_in, gain_attn, w_query, w_keyval, w_out, gain_mlp, w_gate, w_up, w_down):
-    data_index = lax.axis_index("dp")
     local_rows, width = tokens_in.shape
     total_rows = local_rows * lax.axis_size("dp")
-    half_dim = HD // 2
-    frequency = THETA ** (-jnp.arange(half_dim, dtype=jnp.float32) * 2.0 / HD)
-    angles = jnp.arange(total_rows, dtype=jnp.int32).astype(F32)[:, None] * frequency[None, :]
-    cosine, sine = jnp.cos(angles), jnp.sin(angles)
+    frequency = THETA ** (-np.arange(HD // 2) * 2.0 / HD)
+    angles = np.arange(total_rows)[:, None] * frequency[None, :]
+    cosine, sine = np.cos(angles), np.sin(angles)
     attended, full_rows = front(
         tokens_in,
-        gain_attn.reshape(-1, 1, width),
-        jnp.concatenate([cosine, cosine], axis=1),
-        jnp.concatenate([-sine, sine], axis=1),
+        gain_attn.reshape(-1, 128),
+        jnp.asarray(np.concatenate([cosine, cosine], axis=1), F32),
+        jnp.asarray(np.concatenate([-sine, sine], axis=1), F32),
         w_query,
         w_keyval,
         1,
     )
-    cols = w_gate.shape[0]
-    gain = lax.dynamic_slice_in_dim(gain_mlp, data_index * cols, cols, 0)[None, :]
-    return back(attended, full_rows, gain, w_out, w_gate, w_up, w_down, 2)
+    return back(attended, full_rows, gain_mlp.reshape(-1, 128), w_out, w_gate, w_up, w_down, 2)
 
 
 def solution(mesh):

time: 170 us -> 160 us (0.941)
  Pallas kernels: 162 us -> 158 us
  local copies, waits for them, and re-layouts: 4.3 us -> 1.67 us
  other arithmetic: 2.01 us -> 0 us
    pallas_call x1, Pallas kernels: 40.4 us -> 35.5 us  [front(): pl.pallas_call(front_body, out_shape=(jax.ShapeDtypeStruct((parts, local_...]
where the time goes in v3:
time: 160 us
  Pallas kernels  158 us (99%)
  local copies, waits for them, and re-layouts  1.67 us (1%)
    pallas_call x1, Pallas kernels, back(): pl.pallas_call(back_body, out_shape=jax.ShapeDtypeStruct((parts * sub, co...  123 us
    pallas_call x1, Pallas kernels, front(): pl.pallas_call(front_body, out_shape=(jax.ShapeDtypeStruct((parts, local_...  35.5 us

profile of v3, /device:TPU:9, one launch (start us, length us, event | category | flops | bytes accessed | tf_op | source)
XLA Modules:
  0.0 159.9 jit_solution(2760074517668588129)
XLA Ops:
  0.0 35.5 %shard_map.109 = (bf16[4,32,1024]{2,1,0:T(8,128)(2,1)}, bf16[128,8192]{1,0:T(8,128)(2,1)}) custom-call(bf16[128,1024]{1,0:T(8,128)(2,1)} %x_ref.1, bf16[64,128]{1,0:T(8,128)(2,1)} %bitcast.3, f32[512,128]{1,0:T(8,128)} %constant.4.clone.cos_ref, f32[512,128]{1,0:T(8,128)} %constant.5.clone.sin_ref, bf16[8192,1024]{1,0:T(8,128)(2,1)} %wq_hbm.1, ...), custom_call_target="tpu_custom_call" | custom-call | tf_op jit(solution)/shard_map/pallas_call | solution.py:391
  35.5 122.6 %shard_map.110 = bf16[64,2048]{1,0:T(8,128)(2,1)} custom-call(bf16[4,32,1024]{2,1,0:T(8,128)(2,1)} %get-tuple-element.7.att_ref, bf16[128,8192]{1,0:T(8,128)(2,1)} %get-tuple-element.8.rows_ref, bf16[64,128]{1,0:T(8,128)(2,1)} %bitcast.2, bf16[1024,8192]{1,0:T(8,128)(2,1)} %wo_hbm.1, bf16[2048,2048]{1,0:T(8,128)(2,1)} %wg_hbm.1, bf16[2048,2048]{1,0:T(8,128)(2,1)} %wu_hbm.1, ...), custom_call_target="tpu_custom_call" | custom-call | tf_op jit(solution)/shard_map/pallas_call | solution.py:770
  158.2 1.7 %copy.13 = bf16[64,2048]{1,0:T(8,128)(2,1)} copy(bf16[64,2048]{1,0:T(8,128)(2,1)} %shard_map.110) | data formatting | bytes 524288

commit v4 on v3

--- a/solution.py
+++ b/solution.py
@@ -11,7 +11,6 @@
 HD = 128
 EPS = 1e-05
 THETA = 10000.0
-CHUNKS = 2
 TILE = 1024
 GTILE = 512
 PIECES = 2
@@ -20,12 +19,12 @@
     "M0 H2 M1 R0",
     "G0 Z2 U0 H3",
     "R1 G1 Z3 U1",
-    "S0 M2 M3 S1",
-    "R2 G2 U2 D0",
-    "R3 G3 U3 D1",
-    "S2 P0 S3 D2",
-    "P1 D3 V0 W0",
-    "Y0 P2 V1 W1",
+    "S0 M2 S1 D0",
+    "M3 R2 P0 G2",
+    "D1 U2 R3 G3",
+    "U3 S2 P1 V0",
+    "W0 S3 Y0 D2",
+    "D3 P2 V1 W1",
     "Y1 P3 F0 V2",
     "W2 Y2 F1 V3",
     "W3 Y3 F2 F3",
@@ -200,9 +199,9 @@
 
 
 def front_body(
-    x_ref, gain_ref, cos_ref, sin_ref, wq_hbm, wk_hbm, att_ref, full_ref,
-    gain32, blocks, wq, wk, qacc, kacc, stat, kv_src, kv_dst,
-    sem_w, sem_own, sem_t, sem_s, sem_kv, sem_kv_out,
+    x_ref, gain_ref, cos_ref, sin_ref, wq_hbm, wk_hbm, early, att_ref,
+    gain32, blocks, wide, wk, qacc, kacc, stat, kv_src, kv_dst,
+    sem_w, sem_own, sem_t, sem_s, sem_kv, sem_kv_out, after,
 ):
     section, tensor, me = lax.axis_index("section"), lax.axis_index("tensor"), lax.axis_index("dp")
     size_s, size_t, size_d = lax.axis_size("section"), lax.axis_size("tensor"), lax.axis_size("dp")
@@ -222,7 +221,7 @@
         rows = pl.ds(pl.multiple_of((s * size_t + t) * width, width), width)
         loads.append(
             (
-                pltpu.make_async_copy(wq_hbm.at[rows], wq.at[k], sem_w.at[0, k]),
+                pltpu.make_async_copy(wq_hbm.at[rows], wide.at[pl.ds(k * width, width)], sem_w.at[0, k]),
                 pltpu.make_async_copy(wk_hbm.at[rows], wk.at[k], sem_w.at[1, k]),
             )
         )
@@ -256,9 +255,9 @@
         seen.append(k)
         for load in loads[k]:
             load.wait()
+        early(k)
         at = s * size_t + t
         raw = blocks[at]
-        full_ref[:, pl.ds(pl.multiple_of(at * width, width), width)] = raw
         rows = raw.astype(F32)
         part = jnp.sum(rows * rows, axis=-1, keepdims=True)
         stat[...] = part if k == 0 else stat[...] + part
@@ -268,13 +267,15 @@
         @pl.loop(0, qacc.shape[1] // tile)
         def _(j):
             cols = pl.ds(pl.multiple_of(j * tile, tile), tile)
-            term = jnp.dot(scaled, wq[k, :, cols], preferred_element_type=F32)
+            term = jnp.dot(scaled, wide[k * width : (k + 1) * width, cols], preferred_element_type=F32)
             qacc[:, cols] = term if k == 0 else qacc[:, cols] + term
 
         term = jnp.dot(scaled, wk[k], preferred_element_type=F32)
         kacc[...] = term if k == 0 else kacc[...] + term
 
     gather_group(blocks, sem_t, sem_s, on_block)
+    for load in after:
+        load.start()
     factor = lax.rsqrt(stat[...] * (1.0 / features) + EPS)
 
     for i in range(units):
@@ -378,56 +379,14 @@
     each_send(end)
 
 
-def front(tokens, gain, cosine, sine, w_query, w_keyval, collective_id):
-    size_s, size_t, size_d = lax.axis_size("section"), lax.axis_size("tensor"), lax.axis_size("dp")
-    count = size_s * size_t
-    local_rows, width = tokens.shape
-    kv_cols = w_keyval.shape[1]
-    unit = min(kv_cols, HD)
-    pieces = HD // unit
-    rep = (H // KVH) // (w_query.shape[1] // HD)
-    arrivals = 2 * pieces * size_d
-    parts = parts_of(local_rows * size_d // count)
-    return pl.pallas_call(
-        front_body,
-        out_shape=(
-            jax.ShapeDtypeStruct((parts, local_rows // parts, w_query.shape[1]), BF16),
-            jax.ShapeDtypeStruct((local_rows, count * width), BF16),
-        ),
-        in_specs=[VMEM, VMEM, VMEM, VMEM, ANY, ANY],
-        out_specs=(VMEM, VMEM),
-        scratch_shapes=[
-            pltpu.VMEM(gain.shape, F32),
-            pltpu.VMEM((count, local_rows, width), BF16),
-            pltpu.VMEM((count, width, w_query.shape[1]), BF16),
-            pltpu.VMEM((count, width, kv_cols), BF16),
-            pltpu.VMEM((local_rows, w_query.shape[1]), F32),
-            pltpu.VMEM((local_rows, kv_cols), F32),
-            pltpu.VMEM((local_rows, 1), F32),
-            pltpu.VMEM((kv_cols // unit, local_rows, unit), BF16),
-            pltpu.VMEM((2, pieces, local_rows * size_d, unit), BF16),
-            pltpu.SemaphoreType.DMA((2, count)),
-            pltpu.SemaphoreType.DMA,
-            dma_sems((size_t + 1) * PIECES),
-            dma_sems(size_t * (size_s - 1)),
-            dma_sems(arrivals),
-            pltpu.SemaphoreType.DMA((kv_cols // unit * rep * size_d,)),
-        ],
-        compiler_params=pltpu.CompilerParams(
-            collective_id=collective_id, has_side_effects=True, vmem_limit_bytes=66000000
-        ),
-    )(tokens, gain, cosine, sine, w_query, w_keyval)
-
-
 def tile_of(width, most):
     return width if width <= most else most
 
 
 def back_body(
-    att_ref, rows_ref, gain_ref, wo_hbm, wg_hbm, wu_hbm, wd_hbm, out_ref,
-    gain32, wo, wg, wu, wd, att_all, part, pair_rx, comb, z_rx, resid, stat_tx, stat_rx,
+    att_ref, blocks, gain_ref, loads, out_ref, gain32, wo, wide, wd, att_all, part, pair_rx, comb, z_rx, resid, stat_tx, stat_rx,
     nrm, scaled, gu, rx1, tx2, rx2, hid, part2, pair_rx2, comb2, z_rx2,
-    sem_w, sem_att, sem_res, sem_p, sem_z, sem_stat, sem_t, sem_s,
+    sem_att, sem_res, sem_p, sem_z, sem_stat, sem_t, sem_s,
     sem_1, sem_2, sem_h, sem_p2, sem_z2,
 ):
     section, tensor, me = lax.axis_index("section"), lax.axis_index("tensor"), lax.axis_index("dp")
@@ -435,24 +394,17 @@
     group_index = section * size_t + tensor
     parts, dp_sub, width = att_ref.shape
     local_rows = parts * dp_sub
-    features = rows_ref.shape[1]
-    block, cols = resid.shape
+    count, _, span = blocks.shape
+    features = count * span
+    lumps, block, _ = resid.shape
+    cols = lumps * span
     sub = block // parts
     chunks = gu.shape[1]
     dps, sections, tensors = others("dp"), others("section"), others("tensor")
     hops_s = len(sections)
     sends = []
 
-    loads = [
-        pltpu.make_async_copy(wo_hbm.at[:, pl.ds(pl.multiple_of(me * cols, cols), cols)], wo, sem_w.at[0]),
-        pltpu.make_async_copy(wg_hbm, wg, sem_w.at[1]),
-        pltpu.make_async_copy(wu_hbm, wu, sem_w.at[2]),
-        pltpu.make_async_copy(wd_hbm, wd, sem_w.at[3]),
-    ]
-    loads[0].start()
     gain32[...] = gain_ref[...].astype(F32)
-
-    greet(group_peers() + [{"dp": to} for _, to, _ in dps])
 
     def send(copy):
         copy.start()
@@ -478,19 +430,17 @@
     held_rows = pl.ds(pl.multiple_of(lax.rem(group_index, per) * block, block), block)
 
     def resid_copy(step, to):
-        src = rows_ref.at[held_rows, pl.ds(pl.multiple_of(to * cols, cols), cols)]
+        src = blocks.at[pl.ds(to * lumps, lumps), held_rows]
         return push(src, resid, sem_res, step - 1, {"dp": to})
 
     loads[0].wait()
     att_start(1)
-    for load in loads[1:]:
-        load.start()
 
     @pl.when(me == holder)
     def _():
         for step, to, _ in dps:
             resid_copy(step, to).start()
-        resid[...] = rows_ref[held_rows, pl.ds(pl.multiple_of(me * cols, cols), cols)]
+        resid[...] = blocks[pl.ds(me * lumps, lumps), held_rows, :]
 
     for k in range(parts):
         att_all[k, dp_rows(me), :] = att_ref[k]
@@ -572,7 +522,8 @@
                 def _():
                     resid_copy(step, to).wait_recv()
 
-        rows = (resid[k * sub : (k + 1) * sub].astype(F32) + summed).astype(BF16)
+        held = jnp.concatenate([resid[i, k * sub : (k + 1) * sub] for i in range(lumps)], axis=1)
+        rows = (held.astype(F32) + summed).astype(BF16)
         nrm[k, group_rows(section, tensor), :] = rows
         for slot, to in z_sends:
             send(pass_copy(k, slot, tensor, to))
@@ -642,17 +593,18 @@
 
     def gate_up(k):
         if k == 0:
-            loads[1].wait()
-            loads[2].wait()
+            for load in loads[2:]:
+                load.wait()
         scale(k)
         for c in range(chunks):
             @pl.loop(0, share // gtile)
             def _(j):
-                src = pl.ds(pl.multiple_of(c * share + j * gtile, gtile), gtile)
                 lo = pl.ds(pl.multiple_of(j * gtile, gtile), gtile)
                 hi = pl.ds(pl.multiple_of(share + j * gtile, gtile), gtile)
-                gu[k, c, :, lo] = jnp.dot(scaled[...], wg[:, src], preferred_element_type=F32).astype(BF16)
-                gu[k, c, :, hi] = jnp.dot(scaled[...], wu[:, src], preferred_element_type=F32).astype(BF16)
+                for half, at in enumerate((lo, hi)):
+                    first_row = (half * chunks + c) * cols
+                    weights = wide[first_row : first_row + cols, lo]
+                    gu[k, c, :, at] = jnp.dot(scaled[...], weights, preferred_element_type=F32).astype(BF16)
 
             if square:
                 first = near[c % 2]
@@ -695,7 +647,7 @@
 
     def down_wait(k, c):
         if k == 0 and c == 0:
-            loads[3].wait()
+            loads[1].wait()
         if square:
             two = 1 - c % 2
             arrivals = [(two, near[two]), (2, far_peer)]
@@ -752,14 +704,53 @@
             resid_copy(step, to).wait_send()
 
 
-def back(attended, full_rows, gain, w_out, w_gate, w_up, w_down, collective_id):
+def body(
+    x_ref, gain_a, gain_m, cos_ref, sin_ref, wq_hbm, wk_hbm, wo_hbm, wg_hbm, wu_hbm, wd_hbm, out_ref,
+    att, blocks, wide, wk, wo, wd, sem_load, *rest,
+):
+    me = lax.axis_index("dp")
+    cols, hidden_cols = wg_hbm.shape
+    share = wide.shape[1]
+    chunks = hidden_cols // share
+    late = [
+        pltpu.make_async_copy(wo_hbm.at[:, pl.ds(pl.multiple_of(me * cols, cols), cols)], wo, sem_load.at[0]),
+        pltpu.make_async_copy(wd_hbm, wd, sem_load.at[1]),
+    ]
+    for half, source in enumerate((wg_hbm, wu_hbm)):
+        for c in range(chunks):
+            at = half * chunks + c
+            late.append(
+                pltpu.make_async_copy(
+                    source.at[:, c * share : (c + 1) * share], wide.at[pl.ds(at * cols, cols)], sem_load.at[2 + at]
+                )
+            )
+
+    def early(k):
+        if k in (2, 4):
+            late[k // 2 - 1].start()
+
+    front_body(x_ref, gain_a, cos_ref, sin_ref, wq_hbm, wk_hbm, early, att, rest[0], blocks, wide, wk, *rest[1:12], late[2:])
+    back_body(att, blocks, gain_m, late, out_ref, rest[0], wo, wide, wd, *rest[12:])
+
+
+def layer(tokens, gain_a, gain_m, cosine, sine, w_query, w_keyval, w_out, w_gate, w_up, w_down, collective_id):
     size_s, size_t, size_d = lax.axis_size("section"), lax.axis_size("tensor"), lax.axis_size("dp")
-    parts, dp_sub, width = attended.shape
+    count = size_s * size_t
+    local_rows, width = tokens.shape
+    kv_cols = w_keyval.shape[1]
+    unit = min(kv_cols, HD)
+    pieces = HD // unit
+    rep = (H // KVH) // (w_query.shape[1] // HD)
+    arrivals = 2 * pieces * size_d
+    block = local_rows * size_d // count
+    parts = parts_of(block)
+    dp_sub = local_rows // parts
     rows = dp_sub * size_d
-    sub = rows // (size_s * size_t)
+    sub = block // parts
+    heads_cols = w_query.shape[1]
     cols, wide = w_gate.shape
-    chunks = min(CHUNKS, wide // 128)
-    share = wide // chunks
+    share = heads_cols
+    chunks = wide // share
     slots = 2 if size_d == 4 else size_d - 1
     scatter = [
         pltpu.VMEM((parts, rows, cols), BF16),
@@ -768,19 +759,33 @@
         pltpu.VMEM((parts, size_t - 1, sub, cols), BF16),
     ]
     return pl.pallas_call(
-        back_body,
+        body,
         out_shape=jax.ShapeDtypeStruct((parts * sub, cols), BF16),
-        in_specs=[VMEM, VMEM, VMEM, ANY, ANY, ANY, ANY],
+        in_specs=[VMEM] * 5 + [ANY] * 6,
         out_specs=VMEM,
         scratch_shapes=[
-            pltpu.VMEM(gain.shape, F32),
-            pltpu.VMEM((width, cols), BF16),
-            pltpu.VMEM(w_gate.shape, BF16),
-            pltpu.VMEM(w_up.shape, BF16),
+            pltpu.VMEM((parts, dp_sub, heads_cols), BF16),
+            pltpu.VMEM((count, local_rows, width), BF16),
+            pltpu.VMEM((max(w_query.shape[0], 2 * chunks * cols), share), BF16),
+            pltpu.VMEM((count, width, kv_cols), BF16),
+            pltpu.VMEM((heads_cols, cols), BF16),
             pltpu.VMEM(w_down.shape, BF16),
-            pltpu.VMEM((parts, rows, width), BF16),
+            pltpu.SemaphoreType.DMA((2 + 2 * chunks,)),
+            pltpu.VMEM(gain_a.shape, F32),
+            pltpu.VMEM((local_rows, heads_cols), F32),
+            pltpu.VMEM((local_rows, kv_cols), F32),
+            pltpu.VMEM((local_rows, 1), F32),
+            pltpu.VMEM((kv_cols // unit, local_rows, unit), BF16),
+            pltpu.VMEM((2, pieces, local_rows * size_d, unit), BF16),
+            pltpu.SemaphoreType.DMA((2, count)),
+            pltpu.SemaphoreType.DMA,
+            dma_sems((size_t + 1) * PIECES),
+            dma_sems(size_t * (size_s - 1)),
+            dma_sems(arrivals),
+            pltpu.SemaphoreType.DMA((kv_cols // unit * rep * size_d,)),
+            pltpu.VMEM((parts, rows, heads_cols), BF16),
             *scatter,
-            pltpu.VMEM((parts * sub, cols), BF16),
+            pltpu.VMEM((cols // width, block, width), BF16),
             pltpu.VMEM((parts, rows, 128), F32),
             pltpu.VMEM((parts, size_d - 1, dp_sub, 128), F32),
             pltpu.VMEM((parts, rows, cols), BF16),
@@ -791,7 +796,6 @@
             pltpu.VMEM((parts, chunks, dp_sub, 2 * share), BF16),
             pltpu.VMEM((parts, chunks, rows, share), BF16),
             *scatter,
-            pltpu.SemaphoreType.DMA((4,)),
             dma_sems(parts * (size_d - 1)),
             dma_sems(size_d - 1),
             dma_sems(parts * (size_s - 1) * size_t),
@@ -808,7 +812,7 @@
         compiler_params=pltpu.CompilerParams(
             collective_id=collective_id, has_side_effects=True, vmem_limit_bytes=66000000
         ),
-    )(attended, full_rows, gain, w_out, w_gate, w_up, w_down)
+    )(tokens, gain_a, gain_m, cosine, sine, w_query, w_keyval, w_out, w_gate, w_up, w_down)
 
 
 def shards(tokens_in, gain_attn, w_query, w_keyval, w_out, gain_mlp, w_gate, w_up, w_down):
@@ -817,16 +821,20 @@
     frequency = THETA ** (-np.arange(HD // 2) * 2.0 / HD)
     angles = np.arange(total_rows)[:, None] * frequency[None, :]
     cosine, sine = np.cos(angles), np.sin(angles)
-    attended, full_rows = front(
+    return layer(
         tokens_in,
         gain_attn.reshape(-1, 128),
+        gain_mlp.reshape(-1, 128),
         jnp.asarray(np.concatenate([cosine, cosine], axis=1), F32),
         jnp.asarray(np.concatenate([-sine, sine], axis=1), F32),
         w_query,
         w_keyval,
+        w_out,
+        w_gate,
+        w_up,
+        w_down,
         1,
     )
-    return back(attended, full_rows, gain_mlp.reshape(-1, 128), w_out, w_gate, w_up, w_down, 2)
 
 
 def solution(mesh):

time: 160 us -> 153 us (0.956)
  Pallas kernels: 158 us -> 150 us
    pallas_call x2 -> x1, Pallas kernels: 158 us -> 150 us  [layer(): pl.pallas_call(body, out_shape=jax.ShapeDtypeStruct((parts * sub, cols),...]
where the time goes in v4:
time: 153 us; the launch traced here: 152 us
  Pallas kernels  150 us (98%)
  local copies, waits for them, and re-layouts  1.67 us (1%)
    pallas_call x1, Pallas kernels, layer(): pl.pallas_call(body, out_shape=jax.ShapeDtypeStruct((parts * sub, cols),...  150 us

profile of v4, /device:TPU:9, one launch (start us, length us, event | category | flops | bytes accessed | tf_op | source)
XLA Modules:
  0.0 151.9 jit_solution(3354165179213553293)
XLA Ops:
  0.0 150.2 %shard_map.109 = bf16[64,2048]{1,0:T(8,128)(2,1)} custom-call(bf16[128,1024]{1,0:T(8,128)(2,1)} %x_ref.1, bf16[64,128]{1,0:T(8,128)(2,1)} %bitcast.2, bf16[64,128]{1,0:T(8,128)(2,1)} %bitcast.3, f32[512,128]{1,0:T(8,128)} %constant.4.clone.cos_ref, f32[512,128]{1,0:T(8,128)} %constant.5.clone.sin_ref, bf16[8192,1024]{1,0:T(8,128)(2,1)} %wq_hbm.1, ...), custom_call_target="tpu_custom_call" | custom-call | tf_op jit(solution)/shard_map/pallas_call | solution.py:761
  150.2 1.7 %copy.13 = bf16[64,2048]{1,0:T(8,128)(2,1)} copy(bf16[64,2048]{1,0:T(8,128)(2,1)} %shard_map.109) | data formatting | bytes 524288

commit v5 on v4

--- a/solution.py
+++ b/solution.py
@@ -12,8 +12,8 @@
 EPS = 1e-05
 THETA = 10000.0
 TILE = 1024
-GTILE = 512
-PIECES = 2
+GTILE = 1024
+PIECES = 4
 ORDER = (
     "H0 Z0 H1 Z1",
     "M0 H2 M1 R0",
@@ -26,8 +26,8 @@
     "W0 S3 Y0 D2",
     "D3 P2 V1 W1",
     "Y1 P3 F0 V2",
-    "W2 Y2 F1 V3",
-    "W3 Y3 F2 F3",
+    "W2 Y2 V3 W3",
+    "Y3 F1 F2 F3",
 )
 MESH = pl.DeviceIdType.MESH
 F32 = jnp.float32

time: 153 us -> 152 us (level)
  no operation moved by 1% of the time
where the time goes in v5:
time: 152 us; the launch traced here: 151 us
  Pallas kernels  149 us (98%)
  local copies, waits for them, and re-layouts  1.67 us (1%)
    pallas_call x1, Pallas kernels, layer(): pl.pallas_call(body, out_shape=jax.ShapeDtypeStruct((parts * sub, cols),...  149 us

profile of v5, /device:TPU:9, one launch (start us, length us, event | category | flops | bytes accessed | tf_op | source)
XLA Modules:
  0.0 150.5 jit_solution(3082049334959074256)
XLA Ops:
  0.0 148.8 %shard_map.109 = bf16[64,2048]{1,0:T(8,128)(2,1)} custom-call(bf16[128,1024]{1,0:T(8,128)(2,1)} %x_ref.1, bf16[64,128]{1,0:T(8,128)(2,1)} %bitcast.2, bf16[64,128]{1,0:T(8,128)(2,1)} %bitcast.3, f32[512,128]{1,0:T(8,128)} %constant.4.clone.cos_ref, f32[512,128]{1,0:T(8,128)} %constant.5.clone.sin_ref, bf16[8192,1024]{1,0:T(8,128)(2,1)} %wq_hbm.1, ...), custom_call_target="tpu_custom_call" | custom-call | tf_op jit(solution)/shard_map/pallas_call | solution.py:761
  148.9 1.7 %copy.13 = bf16[64,2048]{1,0:T(8,128)(2,1)} copy(bf16[64,2048]{1,0:T(8,128)(2,1)} %shard_map.109) | data formatting | bytes 524288
